TPU v7x, 128 devices: a whole 4x4x4 slice. The times are simulated.
128 devices in a mesh: rep: 1, dp: 128 (over x, y, z, core).
Axes of the slice: x: 4, y: 4, z: 4, core: 2. Of those that a mesh axis runs over, the one named last changes fastest.
Arguments:
- x: bfloat16 [128, 2048, 896], P(('rep', 'dp'))
- dy: bfloat16 [128, 2048, 896], P(('rep', 'dp'))
- w_gate: bfloat16 [2, 896, 2560], P(None, 'dp')
- w_up: bfloat16 [2, 896, 2560], P(None, 'dp')
- w_down: bfloat16 [2, 2560, 896], P(None, 'dp')
Outputs:
- output 1: bfloat16 [128, 2048, 896], P(('rep', 'dp'))
- output 2: bfloat16 [2, 896, 2560], P('rep', 'dp')
- output 3: bfloat16 [2, 896, 2560], P('rep', 'dp')
- output 4: bfloat16 [2, 2560, 896], P('rep', 'dp')
All inputs are finite; a program needn't handle non-finite values.
Results may differ from a plain program's by a relative error of at most 0.018.
Values are sent between devices in bfloat16 or wider.
A program may use at most 1.5 GiB of HBM per device.

v0:
```python
import jax
import jax.numpy as jnp
from jax import lax

NAMES = ("w_gate", "w_up", "w_down")


def matmul(a, w):
    return jnp.dot(a, w, preferred_element_type=jnp.float32).astype(jnp.bfloat16)


def normed(h):
    wide = h.astype(jnp.float32)
    scale = lax.rsqrt(jnp.mean(wide**2, -1, keepdims=True) + 1e-6)
    return (wide * scale).astype(jnp.bfloat16)


def layer(h, w):
    a = normed(h)
    gate = jnp.dot(a, w["w_gate"], preferred_element_type=jnp.float32)
    up = jnp.dot(a, w["w_up"], preferred_element_type=jnp.float32)
    return h + matmul((jax.nn.silu(gate) * up).astype(jnp.bfloat16), w["w_down"])


def stack(weights, h):
    for number in range(weights["w_gate"].shape[0]):
        h = layer(h, {name: w[number] for name, w in weights.items()})
    return h


def solution(mesh):
    groups = mesh.shape["rep"]

    def step(x, dy, *weights):
        shape = x.shape
        x, dy = (t.reshape(groups, -1, *t.shape[1:]) for t in (x, dy))

        def of_a_group(x, dy):
            _, back = jax.vjp(stack, dict(zip(NAMES, weights, strict=True)), x)
            by_weights, by_x = back(dy)
            return (by_x, *(by_weights[name] for name in NAMES))

        by_x, *by_weights = jax.vmap(of_a_group)(x, dy)
        return (by_x.reshape(shape), *(t.reshape(-1, *t.shape[2:]) for t in by_weights))

    return step
```

profile of v0, /device:TPU:0, one launch (start us, length us, event | category | flops | bytes accessed | tf_op | source)
XLA Modules:
  0.0 1454.2 jit_solution(12006075899111129847)
XLA Ops:
  14.3 6.2 copy.21
  24.0 6.1 copy.22
  30.0 53.3 %all-gather.29.cloned.1.call-done = bf16[1,896,2560]{2,0,1:T(2,128)(2,1)} async-done(((bf16[1,7,2560]{2,0,1:T(2,128)(2,1)}), bf16[1,896,2560]{2,0,1:T(2,128)(2,1)}) %all-gather.29.cloned.1.call-update) | async-done | bytes 4587536 | tf_op jit(solution)/vmap(jvp())/squeeze | solution.py:27
  83.3 18.9 %fusion.63 = f32[2048,2560]{1,0:T(8,128)} fusion(bf16[1,2048,896]{1,2,0:T(8,128)(2,1)} %copy.21, f32[2048]{0:T(1024)S(1)} %bitcast.267, bf16[1,896,2560]{2,0,1:T(2,128)(2,1)} %all-gather.29.cloned.1.call-done), kind=kOutput, calls=%fused_computation.80 | convolution fusion | flops 9400745984 | bytes 29237248 | tf_op jit(solution)/vmap(jvp())/dot_general | solution.py:20
  102.3 52.5 %all-gather.31.cloned.1.call-done = bf16[1,896,2560]{2,0,1:T(2,128)(2,1)} async-done(((bf16[1,7,2560]{2,0,1:T(2,128)(2,1)}), bf16[1,896,2560]{2,0,1:T(2,128)(2,1)}) %all-gather.31.cloned.1.call-update) | async-done | bytes 4587536 | tf_op jit(solution)/vmap(jvp())/squeeze | solution.py:27
  154.8 19.5 %fusion.59 = f32[2048,2560]{1,0:T(8,128)} fusion(bf16[1,2048,896]{1,2,0:T(8,128)(2,1)} %copy.21, f32[2048]{0:T(1024)S(1)} %bitcast.268, bf16[1,896,2560]{2,0,1:T(2,128)(2,1)} %all-gather.31.cloned.1.call-done), kind=kOutput, calls=%fused_computation.76 | convolution fusion | flops 9400745984 | bytes 29237248 | tf_op jit(solution)/vmap(jvp())/dot_general | solution.py:21
  174.2 19.4 %fusion.28 = bf16[2048,2560]{1,0:T(8,128)(2,1)} fusion(f32[2048,2560]{1,0:T(8,128)} %fusion.59, f32[2048,2560]{1,0:T(8,128)} %fusion.63), kind=kLoop, calls=%fused_computation.44 | loop fusion | flops 31457280 | bytes 52428800
  193.6 32.0 %all-gather.33.cloned.1.call-done = bf16[1,2560,896]{2,0,1:T(2,128)(2,1)} async-done(((bf16[1,20,896]{2,0,1:T(2,128)(2,1)}), bf16[1,2560,896]{2,0,1:T(2,128)(2,1)}) %all-gather.33.cloned.1.call-update) | async-done | bytes 4587536 | tf_op jit(solution)/vmap(jvp())/squeeze | solution.py:27
  225.7 17.7 %fusion.43 = (f32[2048]{0:T(1024)S(1)}, bf16[1,2048,896]{1,2,0:T(8,128)(2,1)}) fusion(bf16[1,2048,896]{1,2,0:T(8,128)(2,1)} %copy.21, bf16[2048,2560]{1,0:T(8,128)(2,1)} %fusion.28, bf16[1,2560,896]{2,0,1:T(2,128)(2,1)} %all-gather.33.cloned.1.call-done), kind=kOutput, calls=%fused_computation.60 | convolution fusion | flops 9404413952 | bytes 22421504 | tf_op jit(solution)/vmap(jvp())/dot_general | solution.py:9
  244.0 53.0 %all-gather.35.cloned.1.call-done = bf16[1,896,2560]{2,0,1:T(2,128)(2,1)} async-done(((bf16[1,7,2560]{2,0,1:T(2,128)(2,1)}), bf16[1,896,2560]{2,0,1:T(2,128)(2,1)}) %all-gather.35.cloned.1.call-update) | async-done | bytes 4587536 | tf_op jit(solution)/vmap(jvp())/squeeze | solution.py:27
  297.0 19.0 %fusion.53 = f32[2048,2560]{1,0:T(8,128)} fusion(bf16[1,2048,896]{1,2,0:T(8,128)(2,1)} %get-tuple-element.89, f32[2048]{0:T(1024)S(1)} %bitcast.272, bf16[1,896,2560]{2,0,1:T(2,128)(2,1)} %all-gather.35.cloned.1.call-done), kind=kOutput, calls=%fused_computation.70 | convolution fusion | flops 9400745984 | bytes 29237248 | tf_op jit(solution)/vmap(jvp())/dot_general | solution.py:20
  316.0 51.7 %all-gather.37.cloned.1.call-done = bf16[1,2560,896]{2,0,1:T(2,128)(2,1)} async-done(((bf16[1,20,896]{2,0,1:T(2,128)(2,1)}), bf16[1,2560,896]{2,0,1:T(2,128)(2,1)}) %all-gather.37.cloned.1.call-update) | async-done | bytes 4587536 | tf_op jit(solution)/vmap(jvp())/squeeze | solution.py:27
  367.7 17.5 %convolution_convert_fusion.1 = bf16[2048,2560]{1,0:T(8,128)(2,1)} fusion(bf16[1,2560,896]{2,0,1:T(2,128)(2,1)} %all-gather.37.cloned.1.call-done, bf16[1,2048,896]{2,1,0:T(8,128)(2,1)} %param), kind=kOutput, calls=%fused_computation.43 | convolution fusion | flops 9400483840 | bytes 18743296 | tf_op jit(solution)/vmap(transpose(jvp()))/dot_general | solution.py:9
  385.2 19.1 %fusion.24 = f32[2560,896]{0,1:T(8,128)} fusion(bf16[2048,2560]{1,0:T(8,128)(2,1)} %convolution_convert_fusion.1, f32[2048,2560]{1,0:T(8,128)} %fusion.53, bf16[1,2048,896]{1,2,0:T(8,128)(2,1)} %get-tuple-element.89, f32[2048]{0:T(1024)S(1)} %bitcast.273), kind=kOutput, calls=%fused_computation.32 | convolution fusion | flops 9432203264 | bytes 44310528 | tf_op jit(solution)/vmap(transpose(jvp()))/dot_general | solution.py:21
  404.3 34.7 %all-gather.39.cloned.1.call-done = bf16[1,896,2560]{2,0,1:T(2,128)(2,1)} async-done(((bf16[1,7,2560]{2,0,1:T(2,128)(2,1)}), bf16[1,896,2560]{2,0,1:T(2,128)(2,1)}) %all-gather.39.cloned.1.call-update) | async-done | bytes 4587536 | tf_op jit(solution)/vmap(jvp())/squeeze | solution.py:27
  439.0 19.4 %fusion.46 = f32[2048,2560]{1,0:T(8,128)} fusion(bf16[1,2048,896]{1,2,0:T(8,128)(2,1)} %get-tuple-element.89, f32[2048]{0:T(1024)S(1)} %bitcast.274, bf16[1,896,2560]{2,0,1:T(2,128)(2,1)} %all-gather.39.cloned.1.call-done), kind=kOutput, calls=%fused_computation.63 | convolution fusion | flops 9400745984 | bytes 29237248 | tf_op jit(solution)/vmap(jvp())/dot_general | solution.py:21
  458.5 20.7 %fusion.8 = bf16[2048,2560]{1,0:T(8,128)(2,1)} fusion(f32[2048,2560]{1,0:T(8,128)} %fusion.53, f32[2048,2560]{1,0:T(8,128)} %fusion.46, bf16[2048,2560]{1,0:T(8,128)(2,1)S(1)} %copy-done.5), kind=kLoop, calls=%fused_computation.10 | loop fusion | flops 62914560 | bytes 62914560
  479.1 15.0 %fusion.90 = f32[2560,896]{0,1:T(8,128)} fusion(bf16[2048,2560]{1,0:T(8,128)(2,1)} %fusion.8, bf16[1,2048,896]{1,2,0:T(8,128)(2,1)S(1)} %copy-done.7, f32[2048]{0:T(1024)S(1)} %bitcast.275), kind=kOutput, calls=%fused_computation.95 | convolution fusion | flops 9400745984 | bytes 23339008 | tf_op jit(solution)/vmap(transpose(jvp()))/dot_general | solution.py:20
  494.2 14.6 %fusion.51 = bf16[2048,896]{0,1:T(8,128)(2,1)} fusion(bf16[2048,2560]{1,0:T(8,128)(2,1)S(1)} %copy-done.6, bf16[1,896,2560]{2,0,1:T(2,128)(2,1)} %all-gather.35.cloned.1.call-done), kind=kOutput, calls=%fused_computation.68 | convolution fusion | flops 9395240960 | bytes 18743296 | tf_op jit(solution)/vmap(transpose(jvp()))/dot_general | solution.py:20
  508.8 21.6 %fusion.45 = (f32[2048]{0:T(1024)S(1)}, bf16[2048,896]{0,1:T(8,128)(2,1)}) fusion(bf16[1,2048,896]{1,2,0:T(8,128)(2,1)S(1)} %copy-done.7, bf16[2048,896]{0,1:T(8,128)(2,1)} %fusion.51, bf16[1,896,2560]{2,0,1:T(2,128)(2,1)} %all-gather.39.cloned.1.call-done, bf16[2048,2560]{1,0:T(8,128)(2,1)} %convolution_convert_fusion.1, f32[2048,2560]{1,0:T(8,128)} %fusion.53), kind=kOutput, calls=%fused_computation.62 | convolution fusion | flops 9437706240 | bytes 47063040 | tf_op jit(solution)/vmap(transpose(jvp()))/dot_general | solution.py:21
  530.4 4.7 fusion.68
  537.0 16.9 %convolution_convert_fusion = bf16[2048,2560]{1,0:T(8,128)(2,1)} fusion(bf16[1,2048,896]{1,2,0:T(8,128)(2,1)S(1)} %fusion.68, bf16[1,2560,896]{2,0,1:T(2,128)(2,1)} %all-gather.33.cloned.1.call-done), kind=kOutput, calls=%fused_computation.42 | convolution fusion | flops 9400483840 | bytes 18743296 | tf_op jit(solution)/vmap(transpose(jvp()))/dot_general | solution.py:9
  553.9 19.1 %fusion.20 = f32[2560,896]{0,1:T(8,128)} fusion(bf16[2048,2560]{1,0:T(8,128)(2,1)} %convolution_convert_fusion, f32[2048,2560]{1,0:T(8,128)} %fusion.63, bf16[1,2048,896]{1,2,0:T(8,128)(2,1)} %copy.21, f32[2048]{0:T(1024)S(1)} %bitcast.269), kind=kOutput, calls=%fused_computation.30 | convolution fusion | flops 9432203264 | bytes 44310528 | tf_op jit(solution)/vmap(transpose(jvp()))/dot_general | solution.py:21
  573.0 18.5 %fusion.11 = bf16[2048,2560]{1,0:T(8,128)(2,1)S(1)} fusion(f32[2048,2560]{1,0:T(8,128)} %fusion.63, f32[2048,2560]{1,0:T(8,128)} %fusion.59, bf16[2048,2560]{1,0:T(8,128)(2,1)} %convolution_convert_fusion), kind=kLoop, calls=%fused_computation.13 | loop fusion | flops 62914560 | bytes 62914560
  591.5 3.9 copy-done.4
  595.4 12.6 fusion.85
  608.0 412.5 %fusion.115 = (f32[2560,8]{0,1:T(8,128)S(1)}, f32[2560,8]{0,1:T(8,128)S(1)}, f32[2560,8]{0,1:T(8,128)S(1)}, f32[2560,8]{0,1:T(8,128)S(1)}) fusion(f32[2560,896]{0,1:T(8,128)} %fusion.85, f32[2560,896]{0,1:T(8,128)} %fusion.90, f32[2560,896]{0,1:T(8,128)} %fusion.20, f32[2560,896]{0,1:T(8,128)} %fusion.24), kind=kCustom, calls=%all-reduce-scatter.4 | all-reduce-scatter fusion | flops 10485761 | bytes 37027840
  1027.3 15.1 %fusion.61 = bf16[2048,896]{0,1:T(8,128)(2,1)S(1)} fusion(bf16[2048,2560]{1,0:T(8,128)(2,1)} %copy-done.4, bf16[1,896,2560]{2,0,1:T(2,128)(2,1)} %all-gather.29.cloned.1.call-done), kind=kOutput, calls=%fused_computation.78 | convolution fusion | flops 9395240960 | bytes 18743296 | tf_op jit(solution)/vmap(transpose(jvp()))/dot_general | solution.py:20
  1042.4 19.1 %fusion.42 = (f32[2048]{0:T(1024)S(1)}, bf16[2048,896]{0,1:T(8,128)(2,1)}) fusion(bf16[1,2048,896]{1,2,0:T(8,128)(2,1)S(1)} %copy-done.1, bf16[2048,896]{0,1:T(8,128)(2,1)S(1)} %fusion.61, bf16[1,896,2560]{2,0,1:T(2,128)(2,1)} %all-gather.31.cloned.1.call-done, bf16[2048,2560]{1,0:T(8,128)(2,1)} %convolution_convert_fusion, f32[2048,2560]{1,0:T(8,128)} %fusion.63), kind=kOutput, calls=%fused_computation.59 | convolution fusion | flops 9437706240 | bytes 47063040 | tf_op jit(solution)/vmap(transpose(jvp()))/dot_general | solution.py:21
  1066.8 22.5 %fusion.30 = f32[2560,896]{1,0:T(8,128)} fusion(f32[2048,2560]{1,0:T(8,128)} %fusion.46, f32[2048,2560]{1,0:T(8,128)} %fusion.53, bf16[1,2048,896]{2,1,0:T(8,128)(2,1)} %param), kind=kOutput, calls=%fused_computation.46 | convolution fusion | flops 9426698240 | bytes 54788096 | tf_op jit(solution)/vmap(transpose(jvp()))/dot_general | solution.py:9
  1095.8 17.1 %fusion.69 = f32[896,2560]{0,1:T(8,128)} fusion(bf16[2048,2560]{1,0:T(8,128)(2,1)} %fusion.28, bf16[1,2048,896]{1,2,0:T(8,128)(2,1)} %copy-done.3), kind=kOutput, calls=%fused_computation.86 | convolution fusion | flops 9395240960 | bytes 23330816 | tf_op jit(solution)/vmap(transpose(jvp()))/dot_general | solution.py:9
  1112.9 27.4 %collective-permute-start.42 = (bf16[2560,8]{0,1:T(8,128)(2,1)S(1)}, bf16[2560,8]{0,1:T(8,128)(2,1)S(1)}, u32[]{:S(2)}, u32[]{:S(2)}) collective-permute-start(bf16[2560,8]{0,1:T(8,128)(2,1)S(1)} %convert.170), channel_id=1, source_target_pairs={{0,11},{1,12},{2,13},{3,14},{4,15},{5,16},{6,17},{7,18},{8,19},{9,... | collective-permute-start | bytes 122888
  1140.3 4.9 collective-permute-start.43
  1147.4 4.4 collective-permute-start.45
  1153.3 133.9 %all-reduce.19 = (bf16[896,2560]{0,1:T(8,128)(2,1)}, bf16[2560,896]{1,0:T(8,128)(2,1)}) all-reduce(f32[896,2560]{0,1:T(8,128)} %fusion.69, f32[2560,896]{1,0:T(8,128)} %fusion.30), channel_id=29, replica_groups=mesh['axis_0'=128] {'axis_0'}, use_global_device_ids=true, to_apply=%add.5.clone.clone | all-reduce | flops 4587520 | bytes 27525120
  1291.4 4.3 collective-permute-start.50
  1295.7 4.0 collective-permute-start.51
  1309.2 3.9 collective-permute-start.55
  1318.6 9.0 fusion.67
  1327.6 5.2 collective-permute-start.58
  1332.8 4.6 collective-permute-start.59
  1337.4 4.0 collective-permute-start.60
  1341.4 7.5 collective-permute-start.61
  1359.2 5.8 collective-permute-start.11
  1377.3 3.5 collective-permute-start.4
  1381.5 6.0 copy.23
  1390.1 3.8 collective-permute-start.5
  1408.0 5.2 collective-permute-start.18
  (189 shorter events, 127.5 us)
Async XLA Ops:
  7.2 76.2 %all-gather.29.cloned.1.call-start = ((), (), s32[]{:S(2)}) async-start(), calls=%async_computation | async-start | bytes 9246720 | tf_op jit(solution)/vmap(jvp())/squeeze | solution.py:27
  9.0 145.8 %all-gather.31.cloned.1.call-start = ((), (), s32[]{:S(2)}) async-start(), calls=%async_computation.1 | async-start | bytes 9246720 | tf_op jit(solution)/vmap(jvp())/squeeze | solution.py:27
  10.8 214.9 %all-gather.33.cloned.1.call-start = ((), (), s32[]{:S(2)}) async-start(), calls=%async_computation.2 | async-start | bytes 9246720 | tf_op jit(solution)/vmap(jvp())/squeeze | solution.py:27
  12.6 284.4 %all-gather.35.cloned.1.call-start = ((), (), s32[]{:S(2)}) async-start(), calls=%async_computation.3 | async-start | bytes 9246720 | tf_op jit(solution)/vmap(jvp())/squeeze | solution.py:27
  13.2 354.5 %all-gather.37.cloned.1.call-start = ((), (), s32[]{:S(2)}) async-start(), calls=%async_computation.4 | async-start | bytes 9246720 | tf_op jit(solution)/vmap(jvp())/squeeze | solution.py:27
  13.8 425.2 %all-gather.39.cloned.1.call-start = ((), (), s32[]{:S(2)}) async-start(), calls=%async_computation.5 | async-start | bytes 9246720 | tf_op jit(solution)/vmap(jvp())/squeeze | solution.py:27
  1020.5 68.8 %collective-permute-start.32 = (bf16[2560,8]{0,1:T(8,128)(2,1)S(1)}, bf16[2560,8]{0,1:T(8,128)(2,1)S(1)}, u32[]{:S(2)}, u32[]{:S(2)}) collective-permute-start(bf16[2560,8]{0,1:T(8,128)(2,1)S(1)} %convert.170), channel_id=1, source_target_pairs={{0,1},{1,2},{2,3},{3,4},{4,5},{5,6},{6,7},{7,8},{8,9},{9,10},{10,1... | collective-permute-start | bytes 122888
  1021.8 39.8 %collective-permute-start.47 = (bf16[2560,7]{0,1:T(8,128)(2,1)S(1)}, bf16[2560,7]{0,1:T(8,128)(2,1)S(1)}, u32[]{:S(2)}, u32[]{:S(2)}) collective-permute-start(bf16[2560,7]{0,1:T(8,128)(2,1)S(1)} %slice.26), channel_id=1, source_target_pairs={{0,16},{1,17},{2,18},{3,19},{4,20},{5,21},{6,22},{7,23},{8,24},{9,... | collective-permute-start | bytes 107528
  1023.1 39.7 %collective-permute-start.63 = (bf16[2560,7]{0,1:T(8,128)(2,1)S(1)}, bf16[2560,7]{0,1:T(8,128)(2,1)S(1)}, u32[]{:S(2)}, u32[]{:S(2)}) collective-permute-start(bf16[2560,7]{0,1:T(8,128)(2,1)S(1)} %slice.27), channel_id=1, source_target_pairs={{0,16},{1,17},{2,18},{3,19},{4,20},{5,21},{6,22},{7,23},{8,24},{9,... | collective-permute-start | bytes 107528
  1024.4 39.7 %collective-permute-start.15 = (bf16[2560,7]{0,1:T(8,128)(2,1)S(1)}, bf16[2560,7]{0,1:T(8,128)(2,1)S(1)}, u32[]{:S(2)}, u32[]{:S(2)}) collective-permute-start(bf16[2560,7]{0,1:T(8,128)(2,1)S(1)} %slice.24), channel_id=1, source_target_pairs={{0,16},{1,17},{2,18},{3,19},{4,20},{5,21},{6,22},{7,23},{8,24},{9,... | collective-permute-start | bytes 107528
  1025.8 39.7 %collective-permute-start.31 = (bf16[2560,7]{0,1:T(8,128)(2,1)S(1)}, bf16[2560,7]{0,1:T(8,128)(2,1)S(1)}, u32[]{:S(2)}, u32[]{:S(2)}) collective-permute-start(bf16[2560,7]{0,1:T(8,128)(2,1)S(1)} %slice.25), channel_id=1, source_target_pairs={{0,16},{1,17},{2,18},{3,19},{4,20},{5,21},{6,22},{7,23},{8,24},{9,... | collective-permute-start | bytes 107528
  1061.5 29.0 %collective-permute-start.33 = (bf16[2560,8]{0,1:T(8,128)(2,1)S(1)}, bf16[2560,8]{0,1:T(8,128)(2,1)S(1)}, u32[]{:S(2)}, u32[]{:S(2)}) collective-permute-start(bf16[2560,8]{0,1:T(8,128)(2,1)S(1)} %convert.170), channel_id=1, source_target_pairs={{0,2},{1,3},{2,4},{3,5},{4,6},{5,7},{6,8},{7,9},{8,10},{9,11},{10,... | collective-permute-start | bytes 122888
  1062.8 29.0 %collective-permute-start.34 = (bf16[2560,8]{0,1:T(8,128)(2,1)S(1)}, bf16[2560,8]{0,1:T(8,128)(2,1)S(1)}, u32[]{:S(2)}, u32[]{:S(2)}) collective-permute-start(bf16[2560,8]{0,1:T(8,128)(2,1)S(1)} %convert.170), channel_id=1, source_target_pairs={{0,3},{1,4},{2,5},{3,6},{4,7},{5,8},{6,9},{7,10},{8,11},{9,12},{10... | collective-permute-start | bytes 122888
  1064.2 29.0 %collective-permute-start.35 = (bf16[2560,8]{0,1:T(8,128)(2,1)S(1)}, bf16[2560,8]{0,1:T(8,128)(2,1)S(1)}, u32[]{:S(2)}, u32[]{:S(2)}) collective-permute-start(bf16[2560,8]{0,1:T(8,128)(2,1)S(1)} %convert.170), channel_id=1, source_target_pairs={{0,4},{1,5},{2,6},{3,7},{4,8},{5,9},{6,10},{7,11},{8,12},{9,13},{1... | collective-permute-start | bytes 122888
  1065.5 29.0 %collective-permute-start.36 = (bf16[2560,8]{0,1:T(8,128)(2,1)S(1)}, bf16[2560,8]{0,1:T(8,128)(2,1)S(1)}, u32[]{:S(2)}, u32[]{:S(2)}) collective-permute-start(bf16[2560,8]{0,1:T(8,128)(2,1)S(1)} %convert.170), channel_id=1, source_target_pairs={{0,5},{1,6},{2,7},{3,8},{4,9},{5,10},{6,11},{7,12},{8,13},{9,14},{... | collective-permute-start | bytes 122888
  1089.3 23.6 %collective-permute-start.37 = (bf16[2560,8]{0,1:T(8,128)(2,1)S(1)}, bf16[2560,8]{0,1:T(8,128)(2,1)S(1)}, u32[]{:S(2)}, u32[]{:S(2)}) collective-permute-start(bf16[2560,8]{0,1:T(8,128)(2,1)S(1)} %convert.170), channel_id=1, source_target_pairs={{0,6},{1,7},{2,8},{3,9},{4,10},{5,11},{6,12},{7,13},{8,14},{9,15},... | collective-permute-start | bytes 122888
  1090.6 49.7 %collective-permute-start.38 = (bf16[2560,8]{0,1:T(8,128)(2,1)S(1)}, bf16[2560,8]{0,1:T(8,128)(2,1)S(1)}, u32[]{:S(2)}, u32[]{:S(2)}) collective-permute-start(bf16[2560,8]{0,1:T(8,128)(2,1)S(1)} %convert.170), channel_id=1, source_target_pairs={{0,7},{1,8},{2,9},{3,10},{4,11},{5,12},{6,13},{7,14},{8,15},{9,16}... | collective-permute-start | bytes 122888
  1091.9 53.3 %collective-permute-start.39 = (bf16[2560,8]{0,1:T(8,128)(2,1)S(1)}, bf16[2560,8]{0,1:T(8,128)(2,1)S(1)}, u32[]{:S(2)}, u32[]{:S(2)}) collective-permute-start(bf16[2560,8]{0,1:T(8,128)(2,1)S(1)} %convert.170), channel_id=1, source_target_pairs={{0,8},{1,9},{2,10},{3,11},{4,12},{5,13},{6,14},{7,15},{8,16},{9,17... | collective-permute-start | bytes 122888
  1093.2 54.2 %collective-permute-start.40 = (bf16[2560,8]{0,1:T(8,128)(2,1)S(1)}, bf16[2560,8]{0,1:T(8,128)(2,1)S(1)}, u32[]{:S(2)}, u32[]{:S(2)}) collective-permute-start(bf16[2560,8]{0,1:T(8,128)(2,1)S(1)} %convert.170), channel_id=1, source_target_pairs={{0,9},{1,10},{2,11},{3,12},{4,13},{5,14},{6,15},{7,16},{8,17},{9,1... | collective-permute-start | bytes 122888
  1094.5 57.3 %collective-permute-start.41 = (bf16[2560,8]{0,1:T(8,128)(2,1)S(1)}, bf16[2560,8]{0,1:T(8,128)(2,1)S(1)}, u32[]{:S(2)}, u32[]{:S(2)}) collective-permute-start(bf16[2560,8]{0,1:T(8,128)(2,1)S(1)} %convert.170), channel_id=1, source_target_pairs={{0,10},{1,11},{2,12},{3,13},{4,14},{5,15},{6,16},{7,17},{8,18},{9,... | collective-permute-start | bytes 122888
  1112.9 174.3 %collective-permute-start.42 = (bf16[2560,8]{0,1:T(8,128)(2,1)S(1)}, bf16[2560,8]{0,1:T(8,128)(2,1)S(1)}, u32[]{:S(2)}, u32[]{:S(2)}) collective-permute-start(bf16[2560,8]{0,1:T(8,128)(2,1)S(1)} %convert.170), channel_id=1, source_target_pairs={{0,11},{1,12},{2,13},{3,14},{4,15},{5,16},{6,17},{7,18},{8,19},{9,... | collective-permute-start | bytes 122888
  1140.3 148.2 %collective-permute-start.43 = (bf16[2560,8]{0,1:T(8,128)(2,1)S(1)}, bf16[2560,8]{0,1:T(8,128)(2,1)S(1)}, u32[]{:S(2)}, u32[]{:S(2)}) collective-permute-start(bf16[2560,8]{0,1:T(8,128)(2,1)S(1)} %convert.170), channel_id=1, source_target_pairs={{0,12},{1,13},{2,14},{3,15},{4,16},{5,17},{6,18},{7,19},{8,20},{9,... | collective-permute-start | bytes 122888
  1145.2 146.2 %collective-permute-start.44 = (bf16[2560,8]{0,1:T(8,128)(2,1)S(1)}, bf16[2560,8]{0,1:T(8,128)(2,1)S(1)}, u32[]{:S(2)}, u32[]{:S(2)}) collective-permute-start(bf16[2560,8]{0,1:T(8,128)(2,1)S(1)} %convert.170), channel_id=1, source_target_pairs={{0,13},{1,14},{2,15},{3,16},{4,17},{5,18},{6,19},{7,20},{8,21},{9,... | collective-permute-start | bytes 122888
  1147.4 148.3 %collective-permute-start.45 = (bf16[2560,8]{0,1:T(8,128)(2,1)S(1)}, bf16[2560,8]{0,1:T(8,128)(2,1)S(1)}, u32[]{:S(2)}, u32[]{:S(2)}) collective-permute-start(bf16[2560,8]{0,1:T(8,128)(2,1)S(1)} %convert.170), channel_id=1, source_target_pairs={{0,14},{1,15},{2,16},{3,17},{4,18},{5,19},{6,20},{7,21},{8,22},{9,... | collective-permute-start | bytes 122888
  1151.8 147.9 %collective-permute-start.46 = (bf16[2560,8]{0,1:T(8,128)(2,1)S(1)}, bf16[2560,8]{0,1:T(8,128)(2,1)S(1)}, u32[]{:S(2)}, u32[]{:S(2)}) collective-permute-start(bf16[2560,8]{0,1:T(8,128)(2,1)S(1)} %convert.170), channel_id=1, source_target_pairs={{0,15},{1,16},{2,17},{3,18},{4,19},{5,20},{6,21},{7,22},{8,23},{9,... | collective-permute-start | bytes 122888
  1287.2 15.9 %collective-permute-start.48 = (bf16[2560,8]{0,1:T(8,128)(2,1)S(1)}, bf16[2560,8]{0,1:T(8,128)(2,1)S(1)}, u32[]{:S(2)}, u32[]{:S(2)}) collective-permute-start(bf16[2560,8]{0,1:T(8,128)(2,1)S(1)} %convert.171), channel_id=1, source_target_pairs={{0,1},{1,2},{2,3},{3,4},{4,5},{5,6},{6,7},{7,8},{8,9},{9,10},{10,1... | collective-permute-start | bytes 122888
  1288.5 17.9 %collective-permute-start.49 = (bf16[2560,8]{0,1:T(8,128)(2,1)S(1)}, bf16[2560,8]{0,1:T(8,128)(2,1)S(1)}, u32[]{:S(2)}, u32[]{:S(2)}) collective-permute-start(bf16[2560,8]{0,1:T(8,128)(2,1)S(1)} %convert.171), channel_id=1, source_target_pairs={{0,2},{1,3},{2,4},{3,5},{4,6},{5,7},{6,8},{7,9},{8,10},{9,11},{10,... | collective-permute-start | bytes 122888
  1291.4 17.8 %collective-permute-start.50 = (bf16[2560,8]{0,1:T(8,128)(2,1)S(1)}, bf16[2560,8]{0,1:T(8,128)(2,1)S(1)}, u32[]{:S(2)}, u32[]{:S(2)}) collective-permute-start(bf16[2560,8]{0,1:T(8,128)(2,1)S(1)} %convert.171), channel_id=1, source_target_pairs={{0,3},{1,4},{2,5},{3,6},{4,7},{5,8},{6,9},{7,10},{8,11},{9,12},{10... | collective-permute-start | bytes 122888
  1295.7 17.4 %collective-permute-start.51 = (bf16[2560,8]{0,1:T(8,128)(2,1)S(1)}, bf16[2560,8]{0,1:T(8,128)(2,1)S(1)}, u32[]{:S(2)}, u32[]{:S(2)}) collective-permute-start(bf16[2560,8]{0,1:T(8,128)(2,1)S(1)} %convert.171), channel_id=1, source_target_pairs={{0,4},{1,5},{2,6},{3,7},{4,8},{5,9},{6,10},{7,11},{8,12},{9,13},{1... | collective-permute-start | bytes 122888
  1299.7 15.7 %collective-permute-start.52 = (bf16[2560,8]{0,1:T(8,128)(2,1)S(1)}, bf16[2560,8]{0,1:T(8,128)(2,1)S(1)}, u32[]{:S(2)}, u32[]{:S(2)}) collective-permute-start(bf16[2560,8]{0,1:T(8,128)(2,1)S(1)} %convert.171), channel_id=1, source_target_pairs={{0,5},{1,6},{2,7},{3,8},{4,9},{5,10},{6,11},{7,12},{8,13},{9,14},{... | collective-permute-start | bytes 122888
  1303.2 24.4 %collective-permute-start.53 = (bf16[2560,8]{0,1:T(8,128)(2,1)S(1)}, bf16[2560,8]{0,1:T(8,128)(2,1)S(1)}, u32[]{:S(2)}, u32[]{:S(2)}) collective-permute-start(bf16[2560,8]{0,1:T(8,128)(2,1)S(1)} %convert.171), channel_id=1, source_target_pairs={{0,6},{1,7},{2,8},{3,9},{4,10},{5,11},{6,12},{7,13},{8,14},{9,15},... | collective-permute-start | bytes 122888
  1306.5 26.4 %collective-permute-start.54 = (bf16[2560,8]{0,1:T(8,128)(2,1)S(1)}, bf16[2560,8]{0,1:T(8,128)(2,1)S(1)}, u32[]{:S(2)}, u32[]{:S(2)}) collective-permute-start(bf16[2560,8]{0,1:T(8,128)(2,1)S(1)} %convert.171), channel_id=1, source_target_pairs={{0,7},{1,8},{2,9},{3,10},{4,11},{5,12},{6,13},{7,14},{8,15},{9,16}... | collective-permute-start | bytes 122888
  1309.2 28.2 %collective-permute-start.55 = (bf16[2560,8]{0,1:T(8,128)(2,1)S(1)}, bf16[2560,8]{0,1:T(8,128)(2,1)S(1)}, u32[]{:S(2)}, u32[]{:S(2)}) collective-permute-start(bf16[2560,8]{0,1:T(8,128)(2,1)S(1)} %convert.171), channel_id=1, source_target_pairs={{0,8},{1,9},{2,10},{3,11},{4,12},{5,13},{6,14},{7,15},{8,16},{9,17... | collective-permute-start | bytes 122888
  1313.1 28.3 %collective-permute-start.56 = (bf16[2560,8]{0,1:T(8,128)(2,1)S(1)}, bf16[2560,8]{0,1:T(8,128)(2,1)S(1)}, u32[]{:S(2)}, u32[]{:S(2)}) collective-permute-start(bf16[2560,8]{0,1:T(8,128)(2,1)S(1)} %convert.171), channel_id=1, source_target_pairs={{0,9},{1,10},{2,11},{3,12},{4,13},{5,14},{6,15},{7,16},{8,17},{9,1... | collective-permute-start | bytes 122888
  1315.4 33.6 %collective-permute-start.57 = (bf16[2560,8]{0,1:T(8,128)(2,1)S(1)}, bf16[2560,8]{0,1:T(8,128)(2,1)S(1)}, u32[]{:S(2)}, u32[]{:S(2)}) collective-permute-start(bf16[2560,8]{0,1:T(8,128)(2,1)S(1)} %convert.171), channel_id=1, source_target_pairs={{0,10},{1,11},{2,12},{3,13},{4,14},{5,15},{6,16},{7,17},{8,18},{9,... | collective-permute-start | bytes 122888
  1327.6 24.1 %collective-permute-start.58 = (bf16[2560,8]{0,1:T(8,128)(2,1)S(1)}, bf16[2560,8]{0,1:T(8,128)(2,1)S(1)}, u32[]{:S(2)}, u32[]{:S(2)}) collective-permute-start(bf16[2560,8]{0,1:T(8,128)(2,1)S(1)} %convert.171), channel_id=1, source_target_pairs={{0,11},{1,12},{2,13},{3,14},{4,15},{5,16},{6,17},{7,18},{8,19},{9,... | collective-permute-start | bytes 122888
  1332.8 21.4 %collective-permute-start.59 = (bf16[2560,8]{0,1:T(8,128)(2,1)S(1)}, bf16[2560,8]{0,1:T(8,128)(2,1)S(1)}, u32[]{:S(2)}, u32[]{:S(2)}) collective-permute-start(bf16[2560,8]{0,1:T(8,128)(2,1)S(1)} %convert.171), channel_id=1, source_target_pairs={{0,12},{1,13},{2,14},{3,15},{4,16},{5,17},{6,18},{7,19},{8,20},{9,... | collective-permute-start | bytes 122888
  1337.4 18.5 %collective-permute-start.60 = (bf16[2560,8]{0,1:T(8,128)(2,1)S(1)}, bf16[2560,8]{0,1:T(8,128)(2,1)S(1)}, u32[]{:S(2)}, u32[]{:S(2)}) collective-permute-start(bf16[2560,8]{0,1:T(8,128)(2,1)S(1)} %convert.171), channel_id=1, source_target_pairs={{0,13},{1,14},{2,15},{3,16},{4,17},{5,18},{6,19},{7,20},{8,21},{9,... | collective-permute-start | bytes 122888
  1341.4 17.8 %collective-permute-start.61 = (bf16[2560,8]{0,1:T(8,128)(2,1)S(1)}, bf16[2560,8]{0,1:T(8,128)(2,1)S(1)}, u32[]{:S(2)}, u32[]{:S(2)}) collective-permute-start(bf16[2560,8]{0,1:T(8,128)(2,1)S(1)} %convert.171), channel_id=1, source_target_pairs={{0,14},{1,15},{2,16},{3,17},{4,18},{5,19},{6,20},{7,21},{8,22},{9,... | collective-permute-start | bytes 122888
  1349.0 16.1 %collective-permute-start.62 = (bf16[2560,8]{0,1:T(8,128)(2,1)S(1)}, bf16[2560,8]{0,1:T(8,128)(2,1)S(1)}, u32[]{:S(2)}, u32[]{:S(2)}) collective-permute-start(bf16[2560,8]{0,1:T(8,128)(2,1)S(1)} %convert.171), channel_id=1, source_target_pairs={{0,15},{1,16},{2,17},{3,18},{4,19},{5,20},{6,21},{7,22},{8,23},{9,... | collective-permute-start | bytes 122888
  1351.6 16.2 %collective-permute-start = (bf16[2560,8]{0,1:T(8,128)(2,1)S(1)}, bf16[2560,8]{0,1:T(8,128)(2,1)S(1)}, u32[]{:S(2)}, u32[]{:S(2)}) collective-permute-start(bf16[2560,8]{0,1:T(8,128)(2,1)S(1)} %convert.172), channel_id=1, source_target_pairs={{0,1},{1,2},{2,3},{3,4},{4,5},{5,6},{6,7},{7,8},{8,9},{9,10},{10,1... | collective-permute-start | bytes 122888
  1354.3 15.8 %collective-permute-start.1 = (bf16[2560,8]{0,1:T(8,128)(2,1)S(1)}, bf16[2560,8]{0,1:T(8,128)(2,1)S(1)}, u32[]{:S(2)}, u32[]{:S(2)}) collective-permute-start(bf16[2560,8]{0,1:T(8,128)(2,1)S(1)} %convert.172), channel_id=1, source_target_pairs={{0,2},{1,3},{2,4},{3,5},{4,6},{5,7},{6,8},{7,9},{8,10},{9,11},{10,... | collective-permute-start | bytes 122888
  1367.8 22.3 %collective-permute-start.13 = (bf16[2560,8]{0,1:T(8,128)(2,1)S(1)}, bf16[2560,8]{0,1:T(8,128)(2,1)S(1)}, u32[]{:S(2)}, u32[]{:S(2)}) collective-permute-start(bf16[2560,8]{0,1:T(8,128)(2,1)S(1)} %convert.172), channel_id=1, source_target_pairs={{0,14},{1,15},{2,16},{3,17},{4,18},{5,19},{6,20},{7,21},{8,22},{9,... | collective-permute-start | bytes 122888
  1370.1 23.8 %collective-permute-start.14 = (bf16[2560,8]{0,1:T(8,128)(2,1)S(1)}, bf16[2560,8]{0,1:T(8,128)(2,1)S(1)}, u32[]{:S(2)}, u32[]{:S(2)}) collective-permute-start(bf16[2560,8]{0,1:T(8,128)(2,1)S(1)} %convert.172), channel_id=1, source_target_pairs={{0,15},{1,16},{2,17},{3,18},{4,19},{5,20},{6,21},{7,22},{8,23},{9,... | collective-permute-start | bytes 122888
  1371.4 23.8 %collective-permute-start.2 = (bf16[2560,8]{0,1:T(8,128)(2,1)S(1)}, bf16[2560,8]{0,1:T(8,128)(2,1)S(1)}, u32[]{:S(2)}, u32[]{:S(2)}) collective-permute-start(bf16[2560,8]{0,1:T(8,128)(2,1)S(1)} %convert.172), channel_id=1, source_target_pairs={{0,3},{1,4},{2,5},{3,6},{4,7},{5,8},{6,9},{7,10},{8,11},{9,12},{10... | collective-permute-start | bytes 122888
  1374.3 23.4 %collective-permute-start.3 = (bf16[2560,8]{0,1:T(8,128)(2,1)S(1)}, bf16[2560,8]{0,1:T(8,128)(2,1)S(1)}, u32[]{:S(2)}, u32[]{:S(2)}) collective-permute-start(bf16[2560,8]{0,1:T(8,128)(2,1)S(1)} %convert.172), channel_id=1, source_target_pairs={{0,4},{1,5},{2,6},{3,7},{4,8},{5,9},{6,10},{7,11},{8,12},{9,13},{1... | collective-permute-start | bytes 122888
  1377.3 21.7 %collective-permute-start.4 = (bf16[2560,8]{0,1:T(8,128)(2,1)S(1)}, bf16[2560,8]{0,1:T(8,128)(2,1)S(1)}, u32[]{:S(2)}, u32[]{:S(2)}) collective-permute-start(bf16[2560,8]{0,1:T(8,128)(2,1)S(1)} %convert.172), channel_id=1, source_target_pairs={{0,5},{1,6},{2,7},{3,8},{4,9},{5,10},{6,11},{7,12},{8,13},{9,14},{... | collective-permute-start | bytes 122888
  1399.0 16.7 %collective-permute-start.9 = (bf16[2560,8]{0,1:T(8,128)(2,1)S(1)}, bf16[2560,8]{0,1:T(8,128)(2,1)S(1)}, u32[]{:S(2)}, u32[]{:S(2)}) collective-permute-start(bf16[2560,8]{0,1:T(8,128)(2,1)S(1)} %convert.172), channel_id=1, source_target_pairs={{0,10},{1,11},{2,12},{3,13},{4,14},{5,15},{6,16},{7,17},{8,18},{9,... | collective-permute-start | bytes 122888
  (37 other events, 953.6 us)
Sparse Core Ops, SparseCore 0:
  11.0 72.2 all-gather.28
  86.9 67.7 all-gather.30
  157.8 67.7 all-gather.32
  229.1 67.7 all-gather.34
  299.9 67.7 all-gather.36
  371.2 67.7 all-gather.38
where the time goes:
time: 1460 us; the launch traced here: 1450 us
  blocking collectives  546 us (37%)
  matrix products  305 us (21%)
  waiting for transfers between devices  280 us (19%)
  starting transfers between devices  188 us (13%)
  other arithmetic  75.2 us (5%)
  local copies, waits for them, and re-layouts  44.5 us (3%)
  between operations  15.6 us (1%)
    unnamed x2, blocking collectives  546 us
    squeeze x6, waiting for transfers between devices, stack(): h = layer(h, {name: w[number] for name, w in weights.items()})  277 us
    unnamed x64, starting transfers between devices  188 us
    dot_general x6, matrix products, layer(): up = jnp.dot(a, w['w_up'], preferred_element_type=jnp.float32)  118 us
    dot_general x6, matrix products, layer(): gate = jnp.dot(a, w['w_gate'], preferred_element_type=jnp.float32)  95.2 us
    dot_general x5, matrix products, matmul(): jnp.dot(a, w, preferred_element_type=jnp.float32).astype(jnp.bfloat16)  91.7 us
    unnamed x7, other arithmetic  58.5 us
    unnamed x44, local copies, waits for them, and re-layouts  37.5 us
  transfers between devices with their start and end apart: 70, of which 7 were waited for; matrix products, arithmetic and copies ran while one was open for 17% of the time, Pallas kernels for 0%

commit v1 on v0

v1 whole, which is shorter than its diff:
```python
import functools
import jax
import jax.numpy as jnp
from jax import lax
from jax.experimental import pallas as pl
from jax.experimental.pallas import tpu as pltpu
from jax.sharding import PartitionSpec as P

STRIDE = (32, 8, 2)
PIECE = ((8, 2560), (8, 2560), (3, 8, 896))
SPLIT = (1280, 1280, 512)


class Place:
    def __init__(self):
        self.me = lax.axis_index("dp")
        self.core = self.me % 2
        self.at = (self.me // 32, self.me // 8 % 4, self.me // 2 % 4)
        self.partner = self.me + 1 - 2 * self.core

    def beside(self, dim, step):
        here = self.at[dim]
        return self.me + ((here + step) % 4 - here) * STRIDE[dim]

    def greet(self):
        barrier = pltpu.get_barrier_semaphore()
        others = [self.beside(d, s) for d in range(3) for s in (1, 3)] + [self.partner]
        for other in others:
            pl.semaphore_signal(barrier, inc=1, device_id={"dp": other}, device_id_type=pl.DeviceIdType.MESH)
        pl.semaphore_wait(barrier, len(others))


def remote(src, dst, send, recv, to):
    return pltpu.make_async_remote_copy(
        src_ref=src, dst_ref=dst, send_sem=send, recv_sem=recv, device_id={"dp": to}, device_id_type=pl.DeviceIdType.MESH)


def lanes(ref, color, half):
    cut = SPLIT[color]
    span = pl.ds(0, cut) if half == 0 else pl.ds(cut, PIECE[color][-1] - cut)
    return ref.at[:, span] if color < 2 else ref.at[:, :, span]


class Gather:
    SEMS = 24

    def __init__(self, place, color, mine, buf, send, recv, local):
        self.o, self.color, self.mine, self.buf, self.send, self.recv, self.local = place, color, mine, buf, send, recv, local
        self.dims = [(color + n) % 3 for n in range(3)]
        self.q = [place.at[d] for d in self.dims]
        self.sent = []

    def group(self, core, s, j, half=None):
        _, p2, p3 = self.q
        if s == 0:
            ref = self.buf.at[core, p3, p2, j]
            return ref if half is None else lanes(ref, self.color, half)
        lead = (core, p3, j) if s == 1 else (core, j)
        return self.buf.at[lead] if half is None else self.buf.at[(*lead, pl.ds(2 * half, 2))]

    def go(self, n, s, j, half, to, core=None):
        ref = self.group(self.o.core if core is None else core, s, j, half)
        copy = remote(ref, ref, self.send.at[n], self.recv.at[n], to)
        copy.start()
        self.sent.append(copy)

    def landed(self, n, s, j, half, core=None):
        ref = self.group(self.o.core if core is None else core, s, j, half)
        remote(ref, ref, self.send.at[n], self.recv.at[n], self.o.partner).wait_recv()

    def own(self):
        copy = pltpu.make_async_copy(self.mine, self.group(self.o.core, 0, self.q[0]), self.local)
        copy.start()
        copy.wait()

    def first(self, s):
        i, right, left = self.q[s], self.o.beside(self.dims[s], 1), self.o.beside(self.dims[s], 3)
        self.go(4 * s, s, i, None, right)
        self.go(4 * s + 1, s, i, None, left)

    def second(self, s):
        i, right, left = self.q[s], self.o.beside(self.dims[s], 1), self.o.beside(self.dims[s], 3)
        self.landed(4 * s, s, (i + 3) % 4, None)
        self.go(4 * s + 2, s, (i + 3) % 4, 0, right)
        self.landed(4 * s + 1, s, (i + 1) % 4, None)
        self.go(4 * s + 3, s, (i + 1) % 4, 1, left)
        b = 12 + 4 * s
        if s == 0:
            return
        self.go(b, s, (i + 3) % 4, None, self.o.partner)
        self.go(b + 1, s, (i + 1) % 4, None, self.o.partner)

    def third(self, s):
        i = self.q[s]
        self.landed(4 * s + 2, s, (i + 2) % 4, 0)
        self.landed(4 * s + 3, s, (i + 2) % 4, 1)
        b = 12 + 4 * s
        if s == 0:
            self.go(b, 1, self.q[1], None, self.o.partner)
        else:
            self.go(b + 2, s, (i + 2) % 4, None, self.o.partner)

    def finish(self):
        other = 1 - self.o.core
        self.landed(12, 1, self.q[1], None, other)
        for s in (1, 2):
            for n, d in enumerate((3, 1, 2)):
                self.landed(12 + 4 * s + n, s, (self.q[s] + d) % 4, None, other)
        for copy in self.sent:
            copy.wait_send()


def gather_kernel(g, u, d, bg, bu, bd, send, recv, local):
    place = Place()
    gathers = [Gather(place, k, m, b, send.at[k], recv.at[k], local.at[k]) for k, (m, b) in enumerate(zip((g, u, d), (bg, bu, bd)))]
    for one in gathers:
        one.own()
    place.greet()
    for s in range(3):
        for one in gathers:
            one.first(s)
        for one in gathers:
            one.second(s)
        for one in gathers:
            one.third(s)
    for one in gathers:
        one.finish()


def all_gather(g, u, d):
    return pl.pallas_call(
        gather_kernel,
        out_shape=[jax.ShapeDtypeStruct((2, 4, 4, 4, *p), jnp.bfloat16) for p in PIECE],
        in_specs=[pl.BlockSpec(memory_space=pl.ANY)] * 3,
        out_specs=[pl.BlockSpec(memory_space=pltpu.VMEM)] * 3,
        scratch_shapes=[pltpu.SemaphoreType.DMA((3, Gather.SEMS)), pltpu.SemaphoreType.DMA((3, Gather.SEMS)), pltpu.SemaphoreType.DMA((3,))],
        compiler_params=pltpu.CompilerParams(collective_id=0, has_side_effects=True, vmem_limit_bytes=60 * 2**20),
    )(g, u, d)


def in_order(color, buf):
    place = {(color + n) % 3: 3 - n for n in range(3)}
    return buf.transpose(place[0], place[1], place[2], 0, *range(4, buf.ndim))


def by_piece(color, rows):
    d = [(color + n) % 3 for n in range(3)]
    return rows.transpose(3, d[2], d[1], d[0], *range(4, rows.ndim))


def pad_blocks(g, u, d):
    return (jnp.pad(g, ((0, 1), (0, 0))), jnp.pad(u, ((0, 1), (0, 0))), jnp.pad(d, ((0, 4), (0, 0))).reshape(3, 8, 896))


class Scatter:
    SEMS = 16

    def __init__(self, place, color, terms, t, r0, r3, r2, r1, out, send, recv, local):
        self.o, self.color, self.terms, self.t, self.r0, self.r, self.out = place, color, terms, t, r0, (r1, r2, r3), out
        self.send, self.recv, self.local = send, recv, local
        self.dims = [(color + n) % 3 for n in range(3)]
        self.q = [place.at[d] for d in self.dims]
        self.sent = []

    def go(self, n, src, dst, to):
        copy = remote(src, dst, self.send.at[n], self.recv.at[n], to)
        copy.start()
        self.sent.append(copy)

    def landed(self, n, dst):
        remote(dst, dst, self.send.at[n], self.recv.at[n], self.o.partner).wait_recv()

    def exchange(self):
        i = self.q[2]
        self.mine = []
        for n, step in enumerate((2, 1, 3, 0)):
            j = (i + step) % 4
            self.go(n, self.terms.at[1 - self.o.core, j], self.r0.at[j], self.o.partner)
            copy = pltpu.make_async_copy(self.terms.at[self.o.core, j], self.t.at[j], self.local.at[n])
            copy.start()
            self.mine.append(copy)

    def add(self, refs, into, pieces):
        def one(p):
            total = refs[0][p].astype(jnp.float32)
            for ref in refs[1:]:
                total += ref[p].astype(jnp.float32)
            into[p] = total.astype(into.dtype)
        pl.loop(0, pieces)(one)

    def flat(self, ref, n):
        return ref

    def add_cores(self, n):
        i = self.q[2]
        j = (i + (2, 1, 3, 0)[n]) % 4
        self.mine[n].wait()
        self.landed(n, self.r0.at[j])
        for a in range(4):
            self.add([self.t.at[j, a], self.r0.at[j, a]], self.t.at[j, a], 4)

    def group(self, s, j, half=None):
        _, p2, p3 = self.q
        if s == 0:
            ref = self.t.at[p3, p2, j]
            return ref if half is None else lanes(ref, self.color, half)
        lead = (p3, j) if s == 1 else (j,)
        return self.t.at[lead] if half is None else self.t.at[(*lead, pl.ds(2 * half, 2))]

    def slot(self, s, n):
        ref = self.r[s].at[n]
        if n >= 2:
            return ref
        return lanes(ref, self.color, n) if s == 0 else ref.at[pl.ds(2 * n, 2)]

    def first(self, s):
        i, right, left = self.q[s], self.o.beside(self.dims[s], 1), self.o.beside(self.dims[s], 3)
        b = 4 + 4 * s
        self.go(b, self.group(s, (i + 2) % 4, 0), self.slot(s, 0), right)
        self.go(b + 1, self.group(s, (i + 2) % 4, 1), self.slot(s, 1), left)

    def second(self, s):
        i, right, left = self.q[s], self.o.beside(self.dims[s], 1), self.o.beside(self.dims[s], 3)
        b = 4 + 4 * s
        for n, j, to in ((0, (i + 1) % 4, right), (1, (i + 3) % 4, left)):
            self.landed(b + n, self.slot(s, n))
            held, came = self.group(s, j, n), self.slot(s, n)
            if s == 2:
                for a in range(2):
                    self.add([held.at[a], came.at[a]], held.at[a], 4)
            elif s == 1:
                self.add([held, came], held, 2)
            else:
                held[...] = (held[...].astype(jnp.float32) + came[...].astype(jnp.float32)).astype(held.dtype)
            self.go(b + 2 + n, self.group(s, j), self.slot(s, 2 + n), to)

    def third(self, s):
        i = self.q[s]
        b = 4 + 4 * s
        for n in (2, 3):
            self.landed(b + n, self.slot(s, n))
        held, one, two = self.group(s, i), self.slot(s, 2), self.slot(s, 3)
        if s == 2:
            for a in range(4):
                self.add([held.at[a], one.at[a], two.at[a]], held.at[a], 4)
        elif s == 1:
            self.add([held, one, two], held, 4)
        else:
            self.out[...] = (held[...].astype(jnp.float32) + one[...].astype(jnp.float32) + two[...].astype(jnp.float32)).astype(self.out.dtype)

    def finish(self):
        for copy in self.sent:
            copy.wait_send()


def scatter_scratch():
    return [[pltpu.VMEM((*lead, *p), jnp.bfloat16) for p in PIECE] for lead in ((4, 4, 4), (4, 4, 4), (4, 4, 4), (4, 4), (4,))]


def scatter_kernel(g, u, d, og, ou, od, ts, r0s, r3s, r2s, r1s, send, recv, local):
    place = Place()
    all_of = [Scatter(place, k, *a, send.at[k], recv.at[k], local.at[k])
              for k, a in enumerate(zip((g, u, d), ts, r0s, r3s, r2s, r1s, (og, ou, od)))]
    place.greet()
    for one in all_of:
        one.exchange()
    for n in range(4):
        for one in all_of:
            one.add_cores(n)
        if n == 0:
            for one in all_of:
                one.first(2)
    for s in (2, 1, 0):
        for one in all_of:
            if s < 2:
                one.first(s)
        for one in all_of:
            one.second(s)
        for one in all_of:
            one.third(s)
    for one in all_of:
        one.finish()


def reduce_scatter(g, u, d):
    return pl.pallas_call(
        scatter_kernel,
        out_shape=[jax.ShapeDtypeStruct(p, jnp.bfloat16) for p in PIECE],
        in_specs=[pl.BlockSpec(memory_space=pl.ANY)] * 3,
        out_specs=[pl.BlockSpec(memory_space=pltpu.VMEM)] * 3,
        scratch_shapes=[*scatter_scratch(), pltpu.SemaphoreType.DMA((3, Scatter.SEMS)), pltpu.SemaphoreType.DMA((3, Scatter.SEMS)),
                        pltpu.SemaphoreType.DMA((3, 4))],
        compiler_params=pltpu.CompilerParams(collective_id=1, has_side_effects=True, vmem_limit_bytes=60 * 2**20),
    )(g, u, d)


NAMES = ("w_gate", "w_up", "w_down")


def matmul(a, w):
    return jnp.dot(a, w, preferred_element_type=jnp.float32).astype(jnp.bfloat16)


def normed(h):
    wide = h.astype(jnp.float32)
    scale = lax.rsqrt(jnp.mean(wide**2, -1, keepdims=True) + 1e-6)
    return (wide * scale).astype(jnp.bfloat16)


def layer(h, w_gate, w_up, w_down):
    a = normed(h)
    gate = jnp.dot(a, w_gate, preferred_element_type=jnp.float32)
    up = jnp.dot(a, w_up, preferred_element_type=jnp.float32)
    return h + matmul((jax.nn.silu(gate) * up).astype(jnp.bfloat16), w_down)


def whole(bufs):
    g, u, d = (in_order(k, b) for k, b in enumerate(bufs))
    return g[..., :7, :].reshape(896, 2560), u[..., :7, :].reshape(896, 2560), d.reshape(128, 24, 896)[:, :20].reshape(2560, 896)


def pieces(g, u, d):
    cut = lambda k, w, rows: by_piece(k, jnp.pad(w.reshape(4, 4, 4, 2, rows, -1), ((0, 0),) * 4 + ((0, -rows % 8), (0, 0))))
    return cut(0, g, 7), cut(1, u, 7), cut(2, d, 20).reshape(2, 4, 4, 4, 3, 8, 896)


def scattered(terms):
    g, u, d = reduce_scatter(*pieces(*terms))
    return g[:7], u[:7], d.reshape(24, 896)[:20]


def solution(mesh):
    def step(x, dy, w_gate, w_up, w_down):
        h, by_h = x[0], dy[0]
        backs = []
        for n in range(2):
            w = whole(all_gather(*pad_blocks(w_gate[n], w_up[n], w_down[n])))
            h, back = jax.vjp(layer, h, *w)
            backs.append(back)
        sums = [None, None]
        for n in (1, 0):
            by_h, *terms = backs[n](by_h)
            sums[n] = scattered(terms)
        return (by_h[None], *(jnp.stack([sums[0][k], sums[1][k]]) for k in range(3)))

    rows = P(("rep", "dp"))
    weights = [P(None, "dp")] * 3
    return jax.shard_map(step, mesh=mesh, in_specs=(rows, rows, *weights), out_specs=(rows, *weights), check_vma=False)
```

time: 1460 us -> 774 us (0.53)
  blocking collectives: 546 us -> 0 us
  waiting for transfers between devices: 280 us -> 0 us
  Pallas kernels: 0 us -> 230 us
  starting transfers between devices: 188 us -> 0 us
  local copies, waits for them, and re-layouts: 44.5 us -> 193 us
  other arithmetic: 75.2 us -> 12.4 us
  matrix products: 305 us -> 326 us
    unnamed x2 -> x0, blocking collectives: 546 us -> none
    squeeze x6 -> x0, waiting for transfers between devices: 277 us -> none  [stack(): h = layer(h, {name: w[number] for name, w in weights.items()})]
    pallas_call x0 -> x4, Pallas kernels: none -> 230 us  [the longest x2 117 us: reduce_scatter(): pl.pallas_call(scatter_kernel, out_shape=[jax.ShapeDtypeStruct(p, jnp.bfl...]
    unnamed x64 -> x0, starting transfers between devices: 188 us -> none
    reshape x0 -> x16, local copies, waits for them, and re-layouts: none -> 104 us  [the longest x6 45.6 us: pieces(): w.reshape(4, 4, 4, 2, rows, -1)]
    unnamed x7 -> x2, other arithmetic: 58.5 us -> 0.01 us
    transpose x0 -> x6, local copies, waits for them, and re-layouts: none -> 35.4 us  [the longest x4 23.9 us: by_piece(): return rows.transpose(3, d[2], d[1], d[0], *range(4, rows.ndim))]
    slice x3 -> x7, local copies, waits for them, and re-layouts: 5.21 us -> 25.5 us  [the longest x2 11.2 us: whole(): u[..., :7, :].reshape(896, 2560)]
  transfers between devices with their start and end apart: 70 -> 0, of which waited for: 7 -> 0; matrix products, arithmetic and copies ran while one was open for 17% -> 0% of each run, Pallas kernels for 0% -> 0%
where the time goes in v1:
time: 774 us; the launch traced here: 762 us
  matrix products  326 us (42%)
  Pallas kernels  230 us (30%)
  local copies, waits for them, and re-layouts  193 us (25%)
  other arithmetic  12.4 us (2%)
    dot_general x6, matrix products, layer(): up = jnp.dot(a, w_up, preferred_element_type=jnp.float32)  119 us
    pallas_call x2, Pallas kernels, reduce_scatter(): pl.pallas_call(scatter_kernel, out_shape=[jax.ShapeDtypeStruct(p, jnp.bfl...  117 us
    pallas_call x2, Pallas kernels, all_gather(): pl.pallas_call(gather_kernel, out_shape=[jax.ShapeDtypeStruct((2, 4, 4, 4...  113 us
    dot_general x6, matrix products, layer(): gate = jnp.dot(a, w_gate, preferred_element_type=jnp.float32)  110 us
    dot_general x5, matrix products, matmul(): jnp.dot(a, w, preferred_element_type=jnp.float32).astype(jnp.bfloat16)  96.9 us
    reshape x6, local copies, waits for them, and re-layouts, pieces(): w.reshape(4, 4, 4, 2, rows, -1)  45.6 us
    transpose x4, local copies, waits for them, and re-layouts, by_piece(): return rows.transpose(3, d[2], d[1], d[0], *range(4, rows.ndim))  23.9 us
    unnamed x40, local copies, waits for them, and re-layouts  20.9 us

profile of v1, /device:TPU:0, one launch (start us, length us, event | category | flops | bytes accessed | tf_op | source)
XLA Modules:
  0.0 762.4 jit_solution(3629371704122158466)
XLA Ops:
  7.7 6.0 copy.22
  17.2 6.1 copy.21
  23.3 59.1 %shard_map.84 = (bf16[2,4,4,4,8,2560]{5,4,3,2,1,0:T(8,128)(2,1)}, bf16[2,4,4,4,8,2560]{5,4,3,2,1,0:T(8,128)(2,1)}, bf16[2,4,4,4,3,8,896]{6,5,4,3,2,1,0:T(8,128)(2,1)}) custom-call(bf16[8,2560]{1,0:T(8,128)(2,1)} %pad.40.g, bf16[8,2560]{1,0:T(8,128)(2,1)} %pad.41.u, bf16[3,8,896]{2,1,0:T(8,128)(2,1)} %pad_bitcast_fusion.7.d), custom_call_target="tpu_custom_call" | custom-call | tf_op jit(solution)/shard_map/pallas_call | solution.py:131
  82.4 5.5 copy.26
  88.0 7.5 reshape.117
  95.4 5.5 copy.27
  101.0 7.5 reshape.118
  108.5 5.7 copy.28
  114.2 8.0 %reshape.120 = bf16[2560,896]{1,0:T(8,128)(2,1)} reshape(bf16[128,20,896]{2,1,0:T(8,128)(2,1)} %bitcast.114) | data formatting | bytes 9175040 | tf_op jit(solution)/shard_map/reshape | solution.py:319
  122.2 53.5 %shard_map.85 = (bf16[2,4,4,4,8,2560]{5,4,3,2,1,0:T(8,128)(2,1)}, bf16[2,4,4,4,8,2560]{5,4,3,2,1,0:T(8,128)(2,1)}, bf16[2,4,4,4,3,8,896]{6,5,4,3,2,1,0:T(8,128)(2,1)}) custom-call(bf16[8,2560]{1,0:T(8,128)(2,1)} %pad.43.g, bf16[8,2560]{1,0:T(8,128)(2,1)} %pad.44.u, bf16[3,8,896]{2,1,0:T(8,128)(2,1)} %pad_bitcast_fusion.6.d), custom_call_target="tpu_custom_call" | custom-call | tf_op jit(solution)/shard_map/pallas_call | solution.py:131
  175.7 5.6 copy.32
  181.2 7.5 reshape.122
  188.7 5.7 copy.33
  194.5 8.0 %reshape.124 = bf16[2560,896]{1,0:T(8,128)(2,1)} reshape(bf16[128,20,896]{2,1,0:T(8,128)(2,1)} %bitcast.115) | data formatting | bytes 9175040 | tf_op jit(solution)/shard_map/reshape | solution.py:319
  202.4 5.6 copy.35
  208.1 7.5 reshape.125
  215.6 16.5 %convolution_convert_fusion.1 = bf16[2560,2048]{0,1:T(8,128)(2,1)} fusion(bf16[2560,896]{1,0:T(8,128)(2,1)} %reshape.124, bf16[1,2048,896]{2,1,0:T(8,128)(2,1)} %param.6), kind=kOutput, calls=%fused_computation.29 | convolution fusion | flops 9400483840 | bytes 18743296 | tf_op jit(solution)/shard_map/transpose(jvp())/dot_general | solution.py:301
  232.1 17.5 %fusion.40 = f32[2048,2560]{1,0:T(8,128)} fusion(bf16[896,2560]{1,0:T(8,128)(2,1)} %reshape.117, bf16[1,2048,896]{2,1,0:T(8,128)(2,1)S(1)} %copy-done.5, f32[2048]{0:T(1024)S(1)} %fusion.42), kind=kOutput, calls=%fused_computation.70 | convolution fusion | flops 9400745984 | bytes 29237248 | tf_op jit(solution)/shard_map/jvp()/dot_general | solution.py:312
  249.6 26.2 %multiply_convert_fusion.1 = (bf16[2048,2560]{1,0:T(8,128)(2,1)}, f32[2048,2560]{1,0:T(8,128)}) fusion(f32[2048,2560]{1,0:T(8,128)} %fusion.40, bf16[896,2560]{1,0:T(8,128)(2,1)} %reshape.118, bf16[1,2048,896]{2,1,0:T(8,128)(2,1)} %param.5, f32[2048]{0:T(1024)S(1)} %fusion.42), kind=kOutput, calls=%fused_computation.13 | convolution fusion | flops 9432203264 | bytes 60694528 | tf_op jit(solution)/shard_map/jvp()/dot_general | solution.py:313
  275.8 15.0 %fusion.18 = (f32[2048]{0:T(1024)S(1)}, bf16[2048,896]{0,1:T(8,128)(2,1)}) fusion(bf16[2048,2560]{1,0:T(8,128)(2,1)} %get-tuple-element.42, bf16[2560,896]{1,0:T(8,128)(2,1)S(1)} %bitcast.123, bf16[1,2048,896]{1,2,0:T(8,128)(2,1)S(1)} %copy-done), kind=kOutput, calls=%fused_computation.40 | convolution fusion | flops 9404413952 | bytes 22421504 | tf_op jit(solution)/shard_map/jvp()/dot_general | solution.py:301
  290.9 18.0 %fusion.34 = f32[2048,2560]{1,0:T(8,128)} fusion(bf16[896,2560]{1,0:T(8,128)(2,1)} %reshape.125, bf16[2048,896]{0,1:T(8,128)(2,1)} %get-tuple-element.45, f32[2048]{0:T(1024)S(1)} %fusion.43), kind=kOutput, calls=%fused_computation.67 | convolution fusion | flops 9400745984 | bytes 29237248 | tf_op jit(solution)/shard_map/jvp()/dot_general | solution.py:313
  308.9 31.8 %fusion.1 = (bf16[2048,2560]{1,0:T(8,128)(2,1)}, f32[2048,2560]{1,0:T(8,128)}) fusion(f32[2048,2560]{1,0:T(8,128)} %fusion.34, bf16[2560,2048]{0,1:T(8,128)(2,1)} %convolution_convert_fusion.1, bf16[896,2560]{1,0:T(8,128)(2,1)} %reshape.122, bf16[2048,896]{0,1:T(8,128)(2,1)} %get-tuple-element.45, f32[2048]{0:T(1024)S(1)} %fusion.43), kind=kOutput, calls=%fused_computation.5 | convolution fusion | flops 9463660544 | bytes 71180288 | tf_op jit(solution)/shard_map/jvp()/dot_general | solution.py:312
  340.7 21.8 %fusion.23 = bf16[2560,896]{1,0:T(8,128)(2,1)} fusion(f32[2048,2560]{1,0:T(8,128)} %fusion.34, bf16[1,2048,896]{2,1,0:T(8,128)(2,1)} %param.6, f32[2048,2560]{1,0:T(8,128)} %get-tuple-element.47), kind=kOutput, calls=%fused_computation.50 | convolution fusion | flops 9428992000 | bytes 50200576 | tf_op jit(solution)/shard_map/transpose(jvp())/dot_general | solution.py:301
  362.5 18.2 %fusion.7 = bf16[2048,896]{0,1:T(8,128)(2,1)} fusion(bf16[896,2560]{1,0:T(8,128)(2,1)} %reshape.125, bf16[2560,2048]{0,1:T(8,128)(2,1)} %convolution_convert_fusion.1, f32[2048,2560]{1,0:T(8,128)} %get-tuple-element.47), kind=kOutput, calls=%fused_computation.17 | convolution fusion | flops 9426698240 | bytes 39714816 | tf_op jit(solution)/shard_map/transpose(jvp())/dot_general | solution.py:313
  380.7 18.9 %fusion.22 = bf16[896,2560]{1,0:T(8,128)(2,1)} fusion(bf16[2560,2048]{0,1:T(8,128)(2,1)} %convolution_convert_fusion.1, bf16[2048,896]{0,1:T(8,128)(2,1)} %get-tuple-element.45, f32[2048]{0:T(1024)S(1)} %fusion.43, f32[2048,2560]{1,0:T(8,128)} %get-tuple-element.47), kind=kOutput, calls=%fused_computation.49 | convolution fusion | flops 9434497024 | bytes 39723008 | tf_op jit(solution)/shard_map/transpose(jvp())/dot_general | solution.py:313
  399.6 17.1 %fusion.20 = (f32[2048]{0:T(1024)S(1)}, bf16[2048,896]{0,1:T(8,128)(2,1)}) fusion(bf16[2048,896]{0,1:T(8,128)(2,1)} %get-tuple-element.45, bf16[2048,896]{0,1:T(8,128)(2,1)} %fusion.7, bf16[2048,2560]{1,0:T(8,128)(2,1)} %get-tuple-element.46, bf16[896,2560]{1,0:T(8,128)(2,1)} %reshape.122), kind=kOutput, calls=%fused_computation.42 | convolution fusion | flops 9404413952 | bytes 26091520 | tf_op jit(solution)/shard_map/transpose(jvp())/dot_general | solution.py:312
  416.7 14.2 %convolution_convert_fusion.2 = bf16[896,2560]{1,0:T(8,128)(2,1)} fusion(bf16[2048,2560]{1,0:T(8,128)(2,1)} %get-tuple-element.46, bf16[2048,896]{0,1:T(8,128)(2,1)S(1)} %copy-done.6, f32[2048]{0:T(1024)S(1)} %fusion.43), kind=kOutput, calls=%fused_computation.51 | convolution fusion | flops 9400745984 | bytes 18751488 | tf_op jit(solution)/shard_map/transpose(jvp())/dot_general | solution.py:312
  435.8 16.6 %convolution_convert_fusion.3 = bf16[2560,896]{1,0:T(8,128)(2,1)} fusion(bf16[2048,2560]{1,0:T(8,128)(2,1)} %get-tuple-element.42, bf16[2048,896]{0,1:T(8,128)(2,1)S(1)} %fusion.27), kind=kOutput, calls=%fused_computation.52 | convolution fusion | flops 9397534720 | bytes 18743296 | tf_op jit(solution)/shard_map/transpose(jvp())/dot_general | solution.py:301
  452.5 27.0 %fusion.3 = (bf16[2048,2560]{1,0:T(8,128)(2,1)}, bf16[2048,2560]{1,0:T(8,128)(2,1)}) fusion(f32[2048,2560]{1,0:T(8,128)} %fusion.40, f32[2048,2560]{1,0:T(8,128)} %get-tuple-element.43, bf16[2048,896]{0,1:T(8,128)(2,1)S(1)} %fusion.27, bf16[2560,896]{1,0:T(8,128)(2,1)S(1)} %bitcast.125), kind=kOutput, calls=%fused_computation.7 | convolution fusion | flops 9463398400 | bytes 71172096 | tf_op jit(solution)/shard_map/transpose(jvp())/dot_general | solution.py:301
  479.4 18.2 %fusion.9 = bf16[2048,896]{0,1:T(8,128)(2,1)} fusion(bf16[896,2560]{1,0:T(8,128)(2,1)} %reshape.118, bf16[2048,2560]{1,0:T(8,128)(2,1)} %get-tuple-element.51, f32[2048,2560]{1,0:T(8,128)} %fusion.40), kind=kOutput, calls=%fused_computation.19 | convolution fusion | flops 9426698240 | bytes 39714816 | tf_op jit(solution)/shard_map/transpose(jvp())/dot_general | solution.py:313
  497.7 19.1 %fusion.21 = bf16[896,2560]{1,0:T(8,128)(2,1)} fusion(bf16[2048,2560]{1,0:T(8,128)(2,1)} %get-tuple-element.51, bf16[1,2048,896]{1,2,0:T(8,128)(2,1)} %copy.22, f32[2048]{0:T(1024)S(1)} %copy-done.10, f32[2048,2560]{1,0:T(8,128)} %fusion.40), kind=kOutput, calls=%fused_computation.48 | convolution fusion | flops 9434497024 | bytes 39723008 | tf_op jit(solution)/shard_map/transpose(jvp())/dot_general | solution.py:313
  516.8 15.8 %fusion.16 = (f32[2048]{0:T(1024)S(1)}, bf16[2048,896]{0,1:T(8,128)(2,1)S(1)}) fusion(bf16[1,2048,896]{1,2,0:T(8,128)(2,1)} %copy.22, bf16[2048,896]{0,1:T(8,128)(2,1)} %fusion.9, bf16[2048,2560]{1,0:T(8,128)(2,1)} %get-tuple-element.50, bf16[896,2560]{1,0:T(8,128)(2,1)} %reshape.117), kind=kOutput, calls=%fused_computation.38 | convolution fusion | flops 9404413952 | bytes 26091520 | tf_op jit(solution)/shard_map/transpose(jvp())/dot_general | solution.py:312
  532.6 14.1 %convolution_convert_fusion.4 = bf16[896,2560]{1,0:T(8,128)(2,1)} fusion(bf16[2048,2560]{1,0:T(8,128)(2,1)} %get-tuple-element.50, bf16[1,2048,896]{1,2,0:T(8,128)(2,1)S(1)} %copy-done.1, f32[2048]{0:T(1024)S(1)} %copy-done.10), kind=kOutput, calls=%fused_computation.53 | convolution fusion | flops 9400745984 | bytes 18751488 | tf_op jit(solution)/shard_map/transpose(jvp())/dot_general | solution.py:312
  551.4 6.0 copy.42
  557.4 7.4 reshape.126
  564.9 6.0 pad_bitcast_fusion.5.g
  570.8 7.4 reshape.127
  578.3 6.0 pad_bitcast_fusion.4.u
  584.3 7.4 reshape.130
  591.8 5.9 pad_bitcast_fusion.3.g
  597.7 7.4 reshape.131
  605.1 6.0 pad_bitcast_fusion.2.u
  611.1 7.9 %reshape.128 = bf16[4,4,4,2,20,896]{5,4,3,2,1,0:T(8,128)(2,1)} reshape(bf16[2560,896]{1,0:T(8,128)(2,1)} %convolution_convert_fusion.3) | data formatting | bytes 9175040 | tf_op jit(solution)/shard_map/reshape | solution.py:323
  619.0 5.7 copy_bitcast_fusion.1.d
  624.7 59.5 %shard_map.86 = (bf16[8,2560]{1,0:T(8,128)(2,1)}, bf16[8,2560]{1,0:T(8,128)(2,1)}, bf16[3,8,896]{2,1,0:T(8,128)(2,1)}) custom-call(bf16[2,4,4,4,8,2560]{5,4,3,2,1,0:T(8,128)(2,1)} %pad_bitcast_fusion.5.g, bf16[2,4,4,4,8,2560]{5,4,3,2,1,0:T(8,128)(2,1)} %pad_bitcast_fusion.4.u, bf16[2,4,4,4,3,8,896]{6,5,4,3,2,1,0:T(8,128)(2,1)} %copy_bitcast_fusion.1.d), custom_call_target="tpu_custom_call" | custom-call | tf_op jit(solution)/shard_map/pallas_call | solution.py:286
  686.6 7.9 %reshape.132 = bf16[4,4,4,2,20,896]{5,4,3,2,1,0:T(8,128)(2,1)} reshape(bf16[2560,896]{1,0:T(8,128)(2,1)} %fusion.23) | data formatting | bytes 9175040 | tf_op jit(solution)/shard_map/reshape | solution.py:323
  694.5 5.7 copy_bitcast_fusion.d
  700.2 57.5 %shard_map.87 = (bf16[8,2560]{1,0:T(8,128)(2,1)}, bf16[8,2560]{1,0:T(8,128)(2,1)}, bf16[3,8,896]{2,1,0:T(8,128)(2,1)}) custom-call(bf16[2,4,4,4,8,2560]{5,4,3,2,1,0:T(8,128)(2,1)} %pad_bitcast_fusion.3.g, bf16[2,4,4,4,8,2560]{5,4,3,2,1,0:T(8,128)(2,1)} %pad_bitcast_fusion.2.u, bf16[2,4,4,4,3,8,896]{6,5,4,3,2,1,0:T(8,128)(2,1)} %copy_bitcast_fusion.d), custom_call_target="tpu_custom_call" | custom-call | tf_op jit(solution)/shard_map/pallas_call | solution.py:286
  (67 shorter events, 26.9 us)
Async XLA Ops:
  16.6 0.6 copy-start.7
  17.2 232.4 %copy-start.9 = (f32[2048]{0:T(1024)}, f32[2048]{0:T(1024)S(1)}, u32[]{:S(2)}) copy-start(f32[2048]{0:T(1024)S(1)} %fusion.42) | copy-start | bytes 24580
  215.6 16.5 %copy-start.5 = (bf16[1,2048,896]{2,1,0:T(8,128)(2,1)S(1)}, bf16[1,2048,896]{2,1,0:T(8,128)(2,1)}, u32[]{:S(2)}) copy-start(bf16[1,2048,896]{2,1,0:T(8,128)(2,1)} %param.5) | copy-start | bytes 11010052
  232.1 43.7 %slice-start = ((s8[4587520]{0:T(1024)(128)(4,1)}), s8[4194304]{0:T(1024)(128)(4,1)S(1)}, s32[]{:S(2)}) async-start(s8[4587520]{0:T(1024)(128)(4,1)} %bitcast.122), calls=%async_computation | async-start | bytes 8388608
  249.6 26.2 %copy-start = (bf16[1,2048,896]{1,2,0:T(8,128)(2,1)S(1)}, bf16[1,2048,896]{1,2,0:T(8,128)(2,1)}, u32[]{:S(2)}) copy-start(bf16[1,2048,896]{1,2,0:T(8,128)(2,1)} %copy.22) | copy-start | bytes 11010052
  249.6 26.2 %slice-start.1 = ((s8[4587520]{0:T(1024)(128)(4,1)}), s8[393216]{0:T(1024)(128)(4,1)S(1)}, s32[]{:S(2)}) async-start(s8[4587520]{0:T(1024)(128)(4,1)} %bitcast.122), calls=%async_computation.1 | async-start | bytes 786432
  290.9 18.0 %copy-start.11 = (f32[2048]{0:T(1024)}, f32[2048]{0:T(1024)S(1)}, u32[]{:S(2)}) copy-start(f32[2048]{0:T(1024)S(1)} %get-tuple-element.44) | copy-start | bytes 24580
  399.6 17.1 %copy-start.6 = (bf16[2048,896]{0,1:T(8,128)(2,1)S(1)}, bf16[2048,896]{0,1:T(8,128)(2,1)}, u32[]{:S(2)}) copy-start(bf16[2048,896]{0,1:T(8,128)(2,1)} %get-tuple-element.45) | copy-start | bytes 11010052
  416.7 14.2 %copy-start.12 = (f32[2048]{0:T(1024)S(1)}, f32[2048]{0:T(1024)}, u32[]{:S(2)}) copy-start(f32[2048]{0:T(1024)} %copy-done.11) | copy-start | bytes 24580
  416.7 14.2 %copy-start.2 = (bf16[1,2048,896]{1,2,0:T(8,128)(2,1)S(1)}, bf16[1,2048,896]{1,2,0:T(8,128)(2,1)}, u32[]{:S(2)}) copy-start(bf16[1,2048,896]{1,2,0:T(8,128)(2,1)} %copy.21) | copy-start | bytes 11010052
  430.9 21.6 %slice-start.2 = ((s8[4587520]{0:T(1024)(128)(4,1)}), s8[4194304]{0:T(1024)(128)(4,1)S(1)}, s32[]{:S(2)}) async-start(s8[4587520]{0:T(1024)(128)(4,1)} %bitcast.124), calls=%async_computation.2 | async-start | bytes 8388608
  435.8 16.7 %copy-start.3 = (bf16[2048,896]{0,1:T(8,128)(2,1)}, bf16[2048,896]{0,1:T(8,128)(2,1)S(1)}, u32[]{:S(2)}) copy-start(bf16[2048,896]{0,1:T(8,128)(2,1)S(1)} %fusion.27) | copy-start | bytes 11010052
  435.8 16.6 %slice-start.3 = ((s8[4587520]{0:T(1024)(128)(4,1)}), s8[393216]{0:T(1024)(128)(4,1)S(1)}, s32[]{:S(2)}) async-start(s8[4587520]{0:T(1024)(128)(4,1)} %bitcast.124), calls=%async_computation.3 | async-start | bytes 786432
  479.4 18.3 %copy-start.10 = (f32[2048]{0:T(1024)S(1)}, f32[2048]{0:T(1024)}, u32[]{:S(2)}) copy-start(f32[2048]{0:T(1024)} %copy-done.9) | copy-start | bytes 24580
  516.8 15.8 %copy-start.1 = (bf16[1,2048,896]{1,2,0:T(8,128)(2,1)S(1)}, bf16[1,2048,896]{1,2,0:T(8,128)(2,1)}, u32[]{:S(2)}) copy-start(bf16[1,2048,896]{1,2,0:T(8,128)(2,1)} %copy.22) | copy-start | bytes 11010052
  532.6 14.2 %copy-start.8 = (f32[2048]{0:T(1024)S(1)}, f32[2048]{0:T(1024)}, u32[]{:S(2)}) copy-start(f32[2048]{0:T(1024)} %copy-done.7) | copy-start | bytes 24580
  532.6 14.2 %copy-start.4 = (bf16[2048,896]{0,1:T(8,128)(2,1)S(1)}, bf16[2048,896]{0,1:T(8,128)(2,1)}, u32[]{:S(2)}) copy-start(bf16[2048,896]{0,1:T(8,128)(2,1)} %copy-done.3) | copy-start | bytes 11010052

commit v2 on v0

v2 whole, which is shorter than its diff:
```python
import math

import jax
import jax.numpy as jnp
from jax import lax
from jax.experimental import pallas as pl
from jax.experimental.pallas import tpu as pltpu
from jax.sharding import PartitionSpec as P

BF16, F32 = jnp.bfloat16, jnp.float32
D, FF, TOKENS = 896, 2560, 2048
STRIDE = (32, 8, 2)
WIDTHS = ((1024, 768, 768), (768, 1024, 768), (896, 896, 896))
UNITS = [(m, c, c if m == 2 else sum(some[:c]), w) for m, some in enumerate(WIDTHS) for c, w in enumerate(some)]
AFTER, OVER, BEFORE = 1, 2, 3
TORUS = (4, 4, 4)
EDGE = pl.ds(0, 4)
ARRIVE = (BEFORE, AFTER, OVER)


def cut(refs, *sizes):
    refs = list(refs)
    return *[[refs.pop(0) for _ in range(size)] for size in sizes], refs


class Place:
    def __init__(self):
        self.me = lax.axis_index("dp")
        self.core = self.me % 2
        self.at = (self.me // 32, self.me // 8 % 4, self.me // 2 % 4)
        self.partner = self.me + 1 - 2 * self.core

    def beside(self, dim, step):
        here = self.at[dim]
        return self.me + ((here + step) % 4 - here) * STRIDE[dim]

    def greet(self):
        barrier = pltpu.get_barrier_semaphore()
        others = [self.beside(d, s) for d in range(3) for s in (AFTER, BEFORE)] + [self.partner]
        for other in others:
            pl.semaphore_signal(barrier, inc=1, device_id={"dp": other}, device_id_type=pl.DeviceIdType.MESH)
        pl.semaphore_wait(barrier, len(others))


class Ring:
    def __init__(self, place, color, width, send, recv):
        self.o, self.width, self.send, self.recv = place, width, send, recv
        self.dims = [(color + n) % 3 for n in range(3)]
        self.q = [place.at[d] for d in self.dims]

    def copy(self, n, src, dst, to):
        return pltpu.make_async_remote_copy(
            src_ref=src, dst_ref=dst, send_sem=self.send.at[n], recv_sem=self.recv.at[n],
            device_id={"dp": to}, device_id_type=pl.DeviceIdType.MESH)

    def go(self, n, src, dst, to):
        self.copy(n, src, dst, to).start()

    def landed(self, n, dst):
        self.copy(n, dst, dst, self.o.partner).wait_recv()

    def sent(self, n, ref):
        self.copy(n, ref, ref, self.o.partner).wait_send()

    def index(self, s, j, half=None):
        at = [None] * 3
        for n, d in enumerate(self.dims):
            at[d] = EDGE if n < s else j if n == s else self.q[n]
        if half is not None and s:
            at[self.dims[s - 1]] = pl.ds(2 * half, 2)
        return tuple(at)

    def lanes(self, half):
        cut = 512
        return pl.ds(0, cut) if half == 0 else pl.ds(cut, self.width - cut)

    def turn(self, s, step):
        return (self.q[s] + step) % 4

    def sides(self, s):
        return self.q[s], self.o.beside(self.dims[s], AFTER), self.o.beside(self.dims[s], BEFORE)


class Gather(Ring):
    SEMS = 19

    def __init__(self, place, color, width, mine, buf, send, recv, local):
        super().__init__(place, color, width, send, recv)
        self.mine, self.buf, self.local = mine, buf, local

    def group(self, core, s, j, half=None):
        ref = self.buf.at[(*self.index(s, j, half), core)]
        return ref.at[:, self.lanes(half)] if half is not None and s == 0 else ref

    def pass_on(self, n, s, j, half, to):
        ref = self.group(self.o.core, s, j, half)
        self.go(n, ref, ref, to)

    def came(self, n, s, j, half=None, core=None):
        self.landed(n, self.group(self.o.core if core is None else core, s, j, half))

    def load(self):
        pltpu.make_async_copy(self.mine, self.group(self.o.core, 0, self.q[0]), self.local).start()

    def loaded(self):
        pltpu.make_async_copy(self.mine, self.group(self.o.core, 0, self.q[0]), self.local).wait()

    def first(self, s):
        i, right, left = self.sides(s)
        self.pass_on(4 * s, s, i, None, right)
        self.pass_on(4 * s + 1, s, i, None, left)

    def second(self, s):
        i, right, left = self.sides(s)
        self.came(4 * s, s, self.turn(s, BEFORE))
        self.pass_on(4 * s + 2, s, self.turn(s, BEFORE), 0, right)
        self.came(4 * s + 1, s, self.turn(s, AFTER))
        self.pass_on(4 * s + 3, s, self.turn(s, AFTER), 1, left)
        if s:
            b = 10 + 3 * s
            self.pass_on(b, s, self.turn(s, BEFORE), None, self.o.partner)
            self.pass_on(b + 1, s, self.turn(s, AFTER), None, self.o.partner)

    def third(self, s):
        i = self.q[s]
        self.came(4 * s + 2, s, self.turn(s, OVER), 0)
        self.came(4 * s + 3, s, self.turn(s, OVER), 1)
        if s == 0:
            self.pass_on(12, 1, self.q[1], None, self.o.partner)
        else:
            self.pass_on(12 + 3 * s, s, self.turn(s, OVER), None, self.o.partner)

    def finish(self):
        other = 1 - self.o.core
        self.came(12, 1, self.q[1], core=other)
        for s in (1, 2):
            for m, step in enumerate(ARRIVE):
                self.came(10 + 3 * s + m, s, self.turn(s, step), core=other)

    def closed(self):
        for s, i in enumerate(self.q):
            for m, (step, half) in enumerate(((0, None), (0, None), (3, 0), (1, 1))):
                self.sent(4 * s + m, self.group(self.o.core, s, self.turn(s, step), half))
            for m, step in enumerate(ARRIVE if s else ()):
                self.sent(10 + 3 * s + m, self.group(self.o.core, s, self.turn(s, step)))
        self.sent(12, self.group(self.o.core, 1, self.q[1]))


class Scatter(Ring):
    SEMS = 16

    def __init__(self, place, color, width, terms, r0, r3, r2, r1, out, send, recv):
        super().__init__(place, color, width, send, recv)
        self.terms, self.r0, self.r, self.out = terms, r0, (r1, r2, r3), out

    def order(self, n):
        return (self.q[2] + (2, 1, 3, 0)[n]) % 4

    def exchange(self):
        for n in range(4):
            at = self.index(2, self.order(n))
            self.go(n, self.terms.at[(*at, 1 - self.o.core)], self.r0.at[at], self.o.partner)

    def group(self, s, j, half=None):
        ref = self.terms.at[(*self.index(s, j, half), self.o.core)]
        return ref.at[:, self.lanes(half)] if half is not None and s == 0 else ref

    def slot(self, s, n):
        if n >= 2:
            return self.r[s].at[n - 1]
        ref = self.r[s].at[0]
        if s == 0:
            return ref.at[:, self.lanes(n)]
        at = [EDGE] * s
        at[sorted(self.dims[:s]).index(self.dims[s - 1])] = pl.ds(2 * n, 2)
        return ref.at[tuple(at)]

    def add(self, held, others):
        lead = held.shape[:-2]
        if not lead:
            held[...] = sum((o[...].astype(F32) for o in others), held[...].astype(F32)).astype(BF16)
            return

        def one(p):
            at = (p,) if len(lead) == 1 else (p // lead[1], p % lead[1])
            held[at] = sum((o[at].astype(F32) for o in others), held[at].astype(F32)).astype(BF16)

        pl.loop(0, math.prod(lead), unroll=2 if len(lead) == 1 else 4)(one)

    def add_cores(self, n):
        at = self.index(2, self.order(n))
        self.landed(n, self.r0.at[at])
        self.add(self.terms.at[(*at, self.o.core)], [self.r0.at[at]])

    def first(self, s):
        i, right, left = self.sides(s)
        b = 4 + 4 * s
        self.go(b, self.group(s, self.turn(s, OVER), 0), self.slot(s, 0), right)
        self.go(b + 1, self.group(s, self.turn(s, OVER), 1), self.slot(s, 1), left)

    def second(self, s):
        i, right, left = self.sides(s)
        b = 4 + 4 * s
        for n, j, to in ((0, self.turn(s, AFTER), right), (1, self.turn(s, BEFORE), left)):
            self.landed(b + n, self.slot(s, n))
            self.add(self.group(s, j, n), [self.slot(s, n)])
            self.go(b + 2 + n, self.group(s, j), self.slot(s, 2 + n), to)

    def closed(self):
        for n in range(4):
            self.sent(n, self.terms.at[(*self.index(2, self.order(n)), self.o.core)])
        for s, i in enumerate(self.q):
            for m, (step, half) in enumerate(((2, 0), (2, 1), (1, None), (3, None))):
                self.sent(4 + 4 * s + m, self.group(s, self.turn(s, step), half))

    def third(self, s):
        b = 4 + 4 * s
        for n in (2, 3):
            self.landed(b + n, self.slot(s, n))
        held, others = self.group(s, self.q[s]), [self.slot(s, 2), self.slot(s, 3)]
        if s:
            self.add(held, others)
        else:
            self.out[...] = sum((o[...].astype(F32) for o in others), held[...].astype(F32)).astype(BF16)


def block_of(refs, matrix, start, width):
    return refs[matrix].at[start] if matrix == 2 else refs[matrix].at[:, pl.ds(start, width)]


def gathers_of(place, blocks, bufs, send, recv, local):
    return [Gather(place, c, w, block_of(blocks, m, at, w), bufs[n], send.at[n], recv.at[n], local.at[n])
            for n, (m, c, at, w) in enumerate(UNITS)]


def scatters_of(place, terms, r0s, r3s, r2s, r1s, outs, send, recv):
    return [Scatter(place, c, w, terms[n], r0s[n], r3s[n], r2s[n], r1s[n], block_of(outs, m, at, w), send.at[n], recv.at[n])
            for n, (m, c, at, w) in enumerate(UNITS)]


def unit_arrays(*lead):
    return [(*lead, 8, w) for _, _, _, w in UNITS]


def pick(rows, cols, back):
    r = lax.broadcasted_iota(jnp.int32, (rows, cols), 1 if back else 0)
    c = lax.broadcasted_iota(jnp.int32, (rows, cols), 0 if back else 1)
    return ((r == 7 * (c >> 3) + (c & 7)) & ((c & 7) < 7)).astype(F32).astype(BF16)


def dot(a, b, dims=((1,), (0,))):
    return lax.dot_general(a, b, (dims, ((), ())), preferred_element_type=F32)


def unpad(unit, buf, w, wide):
    matrix, _, start, width = UNITS[unit]
    for x in range(4):
        rows = buf[x].astype(F32).reshape(256, width).astype(BF16)
        w[pl.ds(224 * x, 224), pl.ds(start, width)] = dot(wide[...], rows).astype(BF16)


def unpad_down(bufs, w, tall):
    def some(x):
        for i in range(32):
            for r in range(3):
                tall[pl.ds(20 * i + 8 * r, 8), :] = bufs[r][x, i // 8, i // 2 % 4, i % 2].astype(F32)
        w[pl.ds(pl.multiple_of(640 * x, 128), 640), :] = tall[0:640, :].astype(BF16)
    pl.loop(0, 4)(some)

TILE, PART = 512, 1280
TILES, PARTS = TOKENS // TILE, FF // PART
FEW = 512
HERE, VM = pl.BlockSpec(memory_space=pl.ANY), pl.BlockSpec(memory_space=pltpu.VMEM)


def normed(h):
    wide = h.astype(F32)
    scale = lax.rsqrt(jnp.mean(wide**2, -1, keepdims=True) + 1e-6)
    return wide, scale


def gather_semaphores():
    return [pltpu.SemaphoreType.DMA((9, Gather.SEMS)), pltpu.SemaphoreType.DMA((9, Gather.SEMS)), pltpu.SemaphoreType.DMA((9,))]


def up_kernel(x, *refs):
    blocks0, blocks1, (h1, a_out, gate_out, up_out), kept, bufs1, bufs0, w, refs = cut(refs, 3, 3, 4, 3, 9, 9, 3)
    tall, wide, a, act, send0, recv0, local0, send1, recv1, local1, keep = refs
    keeps = [pltpu.make_async_copy(f, t, keep.at[m]) for m, (f, t) in enumerate(zip((*w, a), (*kept, a_out)))]
    rows, part = tiled(TILE, PART)

    def units():
        place = Place()
        return [*gathers_of(place, blocks0, bufs0, send0, recv0, local0), *gathers_of(place, blocks1, bufs1, send1, recv1, local1)]

    def steps(plan, all_of):
        for what, which in zip(plan[::2], plan[1::2]):
            some = [k for k, unit in zip(all_of, "ggguuuddd" + "l" * 9) if unit == which]
            if what == "a":
                for k in some:
                    k.loaded()
                    k.first(0)
                continue
            s = "bdf".find(what) if what in "bdf" else "ceg".find(what)
            for k in some:
                if what in "bdf":
                    k.second(s)
                else:
                    k.third(s)
                    if s < 2:
                        k.first(s + 1)

    def beside(step, plans):
        for n, plan in enumerate(plans):
            if plan:
                pl.when(step == n)(lambda: steps(plan, units()))

    def lanes_of(j):
        return pl.ds(pl.multiple_of(j * PART, PART), PART)

    def rows_of(i):
        return pl.ds(pl.multiple_of(i * TILE, TILE), TILE)

    def ready(matrix):
        for k in first[3 * matrix:3 * matrix + 3]:
            k.finish()
        if matrix == 2:
            unpad_down(bufs0[6:], w[2], tall)
        else:
            for n in range(3 * matrix, 3 * matrix + 3):
                unpad(n, bufs0[n], w[matrix], wide)
        keeps[matrix].start()

    first = units()
    for k in first:
        k.load()
    first[0].o.greet()
    wide[...] = pick(224, 256, False)
    steps("agauad" "bgcgbucudgegbdcddudd" "fgeuedgg", first)
    ready(0)
    steps("fu", first)

    def gate_body(h, out):
        i, j = pl.program_id(0), pl.program_id(1)

        @pl.when(j == 0)
        def _():
            wide_h, scale = normed(h[...])
            a[rows_of(i), :] = (wide_h * scale).astype(BF16)

        beside(i * PARTS + j, ("al", "", "bl", "clfd", "gu", "dl", "el", ""))
        out[...] = dot(a[rows_of(i), :], w[0][:, lanes_of(j)])

    pltpu.emit_pipeline(gate_body, grid=(TILES, PARTS), in_specs=[rows], out_specs=[part])(x, gate_out)
    keeps[3].start()
    ready(1)
    steps("gd", first)

    def up_body(gate, out):
        i, j = pl.program_id(0), pl.program_id(1)
        beside(i * PARTS + j, ("", "", "", "", "", "", "", "fl"))
        up = dot(a[rows_of(i), :], w[1][:, lanes_of(j)])
        out[...] = up
        act[rows_of(i), lanes_of(j)] = (gate[...] * jax.nn.sigmoid(gate[...]) * up).astype(BF16)

    pltpu.emit_pipeline(up_body, grid=(TILES, PARTS), in_specs=[part], out_specs=[part])(gate_out, up_out)
    ready(2)

    def down_body(h, out):
        i = pl.program_id(0)
        beside(i, ("", "", "gl"))
        down = dot(act[rows_of(i), :], w[2][...]).astype(BF16)
        out[...] = (h[...].astype(F32) + down.astype(F32)).astype(BF16)

    tile = pl.BlockSpec((TILE, D), lambda i: (i, 0))
    pltpu.emit_pipeline(down_body, grid=(TILES,), in_specs=[tile], out_specs=[tile])(x, h1)
    for k in first[9:]:
        k.finish()
    for k in first:
        k.closed()
    for k in keeps:
        k.wait()


def params(collective=None):
    return pltpu.CompilerParams(collective_id=collective, has_side_effects=collective is not None, vmem_limit_bytes=67043328)


def tiled(tile, part):
    return pl.BlockSpec((tile, D), lambda i, j: (i, 0)), pl.BlockSpec((tile, part), lambda i, j: (i, j))


def like(shape, dtype=BF16):
    return jax.ShapeDtypeStruct(shape, dtype)


WEIGHTS = ((D, FF), (D, FF), (FF, D))
STATES, HIDDEN = (TOKENS, D), (TOKENS, FF)


def forward(x, blocks0, blocks1):
    units = unit_arrays(*TORUS, 2)
    out = pl.pallas_call(
        up_kernel,
        out_shape=[like(STATES), like(STATES), like(HIDDEN, F32), like(HIDDEN, F32), *map(like, WEIGHTS), *map(like, units)],
        in_specs=[HERE] * 7,
        out_specs=[HERE] * 16,
        scratch_shapes=[
            *[pltpu.VMEM(s, BF16) for s in (*units, *WEIGHTS)],
            pltpu.VMEM((648, D), F32), pltpu.VMEM((224, 256), BF16), pltpu.VMEM(STATES, BF16), pltpu.VMEM(HIDDEN, BF16),
            *gather_semaphores(), *gather_semaphores(), pltpu.SemaphoreType.DMA((4,))],
        compiler_params=params(0),
    )(x, *blocks0, *blocks1)
    return cut(out, *[1] * 4, 3)


def hidden_back(gate, up, by_act):
    sig = jax.nn.sigmoid(gate)
    silu = gate * sig
    by_silu = by_act * up
    by_gate = by_silu * (sig + silu * (1 - sig))
    return (silu * up).astype(BF16), by_gate.astype(BF16), (by_act * silu).astype(BF16)


def norm_back(h, by_h, by_gate_a, by_up_a):
    by_a = (by_gate_a.astype(BF16).astype(F32) + by_up_a.astype(BF16).astype(F32)).astype(BF16).astype(F32)
    wide, scale = normed(h)
    by_scale = jnp.sum(by_a * wide, -1, keepdims=True)
    by_wide = by_a * scale - wide * (by_scale * scale**3 / D)
    return (by_h.astype(F32) + by_wide.astype(BF16).astype(F32)).astype(BF16)


BACK = ((1,), (1,))


def back_part(h, by_h, gate, up, w, lanes, outs, by_in, accs, last):
    by_act = dot(by_h[...], w[2][lanes, :], BACK).astype(BF16).astype(F32)
    for out, value in zip(outs, hidden_back(gate, up, by_act)):
        out[...] = value
    for k, acc in enumerate(accs):
        acc[...] += dot(outs[k + 1][...], w[k][:, lanes], BACK)

    @pl.when(last)
    def _():
        by_in[...] = norm_back(h[...], by_h[...], accs[0][...], accs[1][...])


def top_kernel(*refs):
    bufs, (h, by_h, a), outs, (by_in,), w, accs, (stage, tall, wide, fetch) = cut(refs, 9, 3, 3, 1, 3, 2)
    i, j = pl.program_id(0), pl.program_id(1)

    @pl.when((i == 0) & (j == 0))
    def _():
        held = [stage.at[n % 3, :, :, :, :, :, pl.ds(0, UNITS[n][3])] for n in range(9)]
        copies = [pltpu.make_async_copy(bufs[n], held[n], fetch.at[n % 3]) for n in range(9)]
        for n in range(3):
            copies[n].start()
        wide[...] = pick(224, 256, False)
        for n in range(6):
            copies[n].wait()
            unpad(n, held[n], w[n // 3], wide)
            copies[n + 3].start()
        for n in range(6, 9):
            copies[n].wait()
        unpad_down(held[6:], w[2], tall)

    @pl.when(j == 0)
    def _():
        wide_h, scale = normed(h[...])
        a[...] = (wide_h * scale).astype(BF16)
        for acc in accs:
            acc[...] = jnp.zeros_like(acc)

    lanes = pl.ds(pl.multiple_of(j * PART, PART), PART)
    gate = dot(a[...], w[0][:, lanes])
    up = dot(a[...], w[1][:, lanes])
    back_part(h, by_h, gate, up, w, lanes, outs, by_in, accs, j == PARTS - 1)


def top(h, by_h, bufs):
    rows, part = tiled(TILE, PART)
    return pl.pallas_call(
        top_kernel,
        grid=(TILES, PARTS),
        out_shape=[like(STATES), *[like(HIDDEN)] * 3, like(STATES)],
        in_specs=[*[HERE] * 9, rows, rows],
        out_specs=[rows, part, part, part, rows],
        scratch_shapes=[*[pltpu.VMEM(s, BF16) for s in WEIGHTS], *[pltpu.VMEM((TILE, D), F32)] * 2,
                        pltpu.VMEM((3, 4, 4, 4, 2, 8, 1024), BF16), pltpu.VMEM((648, D), F32), pltpu.VMEM((224, 256), BF16),
                        pltpu.SemaphoreType.DMA((3,))],
        compiler_params=params(),
    )(*bufs, h, by_h)


COLS = 256


def sum_kernel(below, *refs):
    (a, by_h, act, by_gate, by_up), came, outs, gone, refs = cut(refs, 5, 7 * below, 3, 4 * below)
    terms, r0s, r3s, r2s, r1s, refs = cut(refs, *[len(UNITS)] * 5)
    back, send, recv, fetch, fetch_wide, whole = refs
    def all_units():
        return scatters_of(Place(), terms, r0s, r3s, r2s, r1s, outs, send, recv)

    units = all_units()

    def cores(some):
        for n in range(4):
            for k in some:
                k.add_cores(n)
            if not n:
                for k in some:
                    k.first(2)

    def steps(plan, units=units):
        for what, which in zip(plan[::2], plan[1::2]):
            some = [k for k, unit in zip(units, "ggguuuddd") if unit == which]
            if what == "c":
                cores(some)
            for k in some:
                if what == "b":
                    k.second(2)
                elif what == "f":
                    k.third(2)
                    k.first(1)
                elif what == "h":
                    k.second(1)
                elif what == "k":
                    k.third(1)
                    k.first(0)
                elif what == "m":
                    k.second(0)
                elif what == "p":
                    k.third(0)

    units[0].o.greet()
    back[...] = pick(256, 224, True)

    def make_all(side, tall, cols, made):
        def wide_copy(x):
            return pltpu.make_async_copy(act.at[:, pl.ds(pl.multiple_of(640 * x, 128), 640)], cols.at[x % 2], fetch_wide.at[x % 2])

        def copy(src, t):
            return pltpu.make_async_copy(
                src.at[:, pl.ds(pl.multiple_of(COLS * t, COLS), COLS)], cols.at[t % 2, :, pl.ds(0, COLS)], fetch.at[t % 2])

        states = pltpu.make_async_copy(by_h, side, whole)
        states.start()
        wide_copy(0).start()
        states.wait()
        tall[640:648, :] = jnp.zeros((8, D), F32)

        def down(x):
            wide_copy(x).wait()
            pl.when(x < 3)(lambda: wide_copy(x + 1).start())
            tall[0:640, :] = dot(cols[x % 2], side[...], ACROSS)
            for i in range(32):
                for r in range(3):
                    terms[6 + r][x, i // 8, i // 2 % 4, i % 2] = tall[pl.ds(20 * i + 8 * r, 8), :].astype(BF16)

        pl.loop(0, 4)(down)
        states = pltpu.make_async_copy(a, side, whole)
        states.start()
        copy(by_gate, 0).start()
        for k in units[6:]:
            k.exchange()
        states.wait()

        for unit, then in enumerate(("cd", "", "bdcg", "fd", "hdbg", "kdfg")):
            matrix, _, start, width = UNITS[unit]
            src, term = (by_gate, by_up)[matrix], terms[unit]

            def one(n):
                t = start // COLS + n
                copy(src, t).wait()
                pl.when(t < FF // COLS - 1)(lambda: copy(src, t + 1).start())
                lanes = pl.ds(pl.multiple_of(n * COLS, COLS), COLS)
                made[:, lanes] = dot(side[...], cols[t % 2, :, 0:COLS], ACROSS).astype(BF16)

            pl.loop(0, width // COLS)(one)
            for x in range(4):
                term[x] = dot(back[...], made[224 * x:224 * (x + 1), 0:width]).reshape(4, 4, 2, 8, width).astype(BF16)
            if unit == 2:
                copy(by_up, 0).start()
            units[unit].exchange()
            steps(then)

    pl.run_scoped(make_all, pltpu.VMEM(STATES, BF16), pltpu.VMEM((648, D), F32), pltpu.VMEM((2, TOKENS, 640), BF16),
                  pltpu.VMEM((D, 1024), BF16))

    if not below:
        steps("mdcuhgpdkgbumgfupghukumupu")
    else:
        def lower(*refs):
            w, accs = cut(refs, 3)
            loads = [pltpu.make_async_copy(came[k + 4], w[k], fetch.at[0] if not k else fetch_wide.at[k - 1]) for k in range(3)]
            for load in loads:
                load.start()
            steps("mdcu")
            for load in loads:
                load.wait()
            rows, part = tiled(TILE, FEW)
            once = pl.BlockSpec(rows.block_shape, rows.index_map, pipeline_mode=pl.Buffered(1))

            def body(h, by_next, gate, up, act_out, by_gate_out, by_up_out, by_in):
                i, j = pl.program_id(0), pl.program_id(1)
                for n, plan in enumerate(("hgpd", "", "kg", "bu", "mg", "", "pg", "fu", "", "hu", "", "ku", "", "mu", "", "pu")):
                    if plan:
                        pl.when(i * (FF // FEW) + j == n)(lambda: steps(plan, all_units()))

                @pl.when(j == 0)
                def _():
                    for acc in accs:
                        acc[...] = jnp.zeros_like(acc)

                lanes = pl.ds(pl.multiple_of(j * FEW, FEW), FEW)
                back_part(h, by_next, gate[...], up[...], w, lanes, (act_out, by_gate_out, by_up_out), by_in, accs, j == FF // FEW - 1)

            pltpu.emit_pipeline(
                body, grid=(TILES, FF // FEW), in_specs=[once, once, part, part], out_specs=[part, part, part, rows])(*came[:4], *gone)

        pl.run_scoped(lower, *[pltpu.VMEM(s, BF16) for s in WEIGHTS], *[pltpu.VMEM((TILE, D), F32)] * 2)
    for k in units:
        k.closed()


ACROSS = ((0,), (0,))


def summed(a, by_h, act, by_gate, by_up, below=()):
    arrays = lambda *lead: [pltpu.VMEM(s, BF16) for s in unit_arrays(*lead)]
    more = [*[like(HIDDEN)] * 3, like(STATES)] if below else []
    g, u, d, *gone = pl.pallas_call(
        lambda *refs: sum_kernel(bool(below), *refs),
        out_shape=[like((8, FF)), like((8, FF)), like((3, 8, D)), *more],
        in_specs=[HERE] * (5 + len(below)),
        out_specs=[VM] * 3 + [HERE] * len(more),
        scratch_shapes=[
            *arrays(*TORUS, 2), *arrays(*TORUS), *arrays(3, 4, 4), *arrays(3, 4), *arrays(3),
            pltpu.VMEM((256, 224), BF16),
            pltpu.SemaphoreType.DMA((9, Scatter.SEMS)), pltpu.SemaphoreType.DMA((9, Scatter.SEMS)),
            pltpu.SemaphoreType.DMA((2,)), pltpu.SemaphoreType.DMA((2,)), pltpu.SemaphoreType.DMA],
        compiler_params=params(1 + len(below)),
    )(a, by_h, act, by_gate, by_up, *below)
    return (g[:7], u[:7], d.reshape(24, D)[:20]), gone


def pad_blocks(g, u, d):
    return jnp.pad(g, ((0, 1), (0, 0))), jnp.pad(u, ((0, 1), (0, 0))), jnp.pad(d, ((0, 4), (0, 0))).reshape(3, 8, D)


def solution(mesh):
    def step(x, dy, w_gate, w_up, w_down):
        x, dy = x[0], dy[0]
        blocks = [pad_blocks(w_gate[n], w_up[n], w_down[n]) for n in range(2)]
        (h1,), (a0,), (gate,), (up,), w0, bufs1 = forward(x, *blocks)
        a1, act1, by_gate1, by_up1, by_h1 = top(h1, dy, bufs1)
        sums1, (*parts0, by_x) = summed(a1, dy, act1, by_gate1, by_up1, below=(x, by_h1, gate, up, *w0))
        sums0, _ = summed(a0, by_h1, *parts0)
        return (by_x[None], *(jnp.stack([sums0[k], sums1[k]]) for k in range(3)))

    rows = P(("rep", "dp"))
    weights = [P(None, "dp")] * 3
    return jax.shard_map(step, mesh=mesh, in_specs=(rows, rows, *weights), out_specs=(rows, *weights), check_vma=False)
```

time: 1460 us -> 438 us (0.30)
  blocking collectives: 546 us -> 0 us
  Pallas kernels: 0 us -> 414 us
  matrix products: 305 us -> 0 us
  waiting for transfers between devices: 280 us -> 0 us
  starting transfers between devices: 188 us -> 0 us
  other arithmetic: 75.2 us -> 0.06 us
  local copies, waits for them, and re-layouts: 44.5 us -> 18 us
  between operations: 15.6 us -> 0.94 us
    unnamed x2 -> x0, blocking collectives: 546 us -> none
    pallas_call x0 -> x4, Pallas kernels: none -> 414 us  [the longest x2 222 us: summed(): pl.pallas_call(lambda *refs: sum_kernel(bool(below), *refs), out_shape=[l...]
    dot_general x17 -> x0, matrix products: 305 us -> none  [the longest x6 118 us: layer(): up = jnp.dot(a, w['w_up'], preferred_element_type=jnp.float32)]
    squeeze x6 -> x0, waiting for transfers between devices: 277 us -> none  [stack(): h = layer(h, {name: w[number] for name, w in weights.items()})]
    unnamed x64 -> x0, starting transfers between devices: 188 us -> none
    unnamed x7 -> x0, other arithmetic: 58.5 us -> none
    unnamed x44 -> x4, local copies, waits for them, and re-layouts: 37.5 us -> 6.23 us
  transfers between devices with their start and end apart: 70 -> 0, of which waited for: 7 -> 0; matrix products, arithmetic and copies ran while one was open for 17% -> 0% of each run, Pallas kernels for 0% -> 0%
where the time goes in v2:
time: 438 us; the launch traced here: 433 us
  Pallas kernels  414 us (95%)
  local copies, waits for them, and re-layouts  18 us (4%)
    pallas_call x2, Pallas kernels, summed(): pl.pallas_call(lambda *refs: sum_kernel(bool(below), *refs), out_shape=[l...  222 us
    pallas_call x1, Pallas kernels, forward(): pl.pallas_call(up_kernel, out_shape=[like(STATES), like(STATES), like(HID...  113 us
    pallas_call x1, Pallas kernels, top(): pl.pallas_call(top_kernel, grid=(TILES, PARTS), out_shape=[like(STATES),...  79 us

profile of v2, /device:TPU:0, one launch (start us, length us, event | category | flops | bytes accessed | tf_op | source)
XLA Modules:
  0.0 432.6 jit_solution(11373517227373522131)
XLA Ops:
  0.6 1.1 fusion.2
  1.7 0.6 pad.23.refs_3_
  2.4 0.6 pad.20.refs_0_
  3.0 1.1 fusion.1
  4.1 0.6 pad.24.refs_4_
  4.7 0.6 pad.21.refs_1_
  5.4 1.1 fusion
  6.5 0.6 pad_bitcast_fusion.refs_5_
  7.1 0.6 pad_bitcast_fusion.1.refs_2_
  7.7 112.6 %shard_map.84 = (bf16[2048,896]{1,0:T(8,128)(2,1)}, bf16[2048,896]{1,0:T(8,128)(2,1)}, f32[2048,2560]{1,0:T(8,128)}, f32[2048,2560]{1,0:T(8,128)}, bf16[896,2560...) custom-call(bf16[2048,896]{1,0:T(8,128)(2,1)} %bitcast.33, ...), custom_call_target="tpu_custom_call" | custom-call | tf_op jit(solution)/shard_map/pallas_call | solution.py:403
  120.4 79.0 %shard_map.85 = (bf16[2048,896]{1,0:T(8,128)(2,1)}, bf16[2048,2560]{1,0:T(8,128)(2,1)}, bf16[2048,2560]{1,0:T(8,128)(2,1)}, bf16[2048,2560]{1,0:T(8,128)(2,1)}, bf16[2048,896]{1,0:T(8,128)(2,1)}) custom-call(bf16[4,4,4,2,8,1024]{5,4,3,2,1,0:T(8,128)(2,1)} %get-tuple-element.35.refs_0_, bf16[4,4,4,2,8,768]{5,4,3,2,1,0:T(8,128)(2,1)} %get-tuple-element.36.refs_1_, ...), custom_call_target="tpu_custom_call" | custom-call | tf_op jit(solution)/shard_map/pallas_call | solution.py:482
  199.4 131.2 %shard_map.86 = (bf16[8,2560]{1,0:T(8,128)(2,1)}, bf16[8,2560]{1,0:T(8,128)(2,1)}, bf16[3,8,896]{2,1,0:T(8,128)(2,1)}, bf16[2048,2560]{1,0:T(8,128)(2,1)}, bf16[...) custom-call(bf16[2048,896]{1,0:T(8,128)(2,1)} %get-tuple-element.45.refs_0_, ...), custom_call_target="tpu_custom_call" | custom-call | tf_op jit(solution)/shard_map/pallas_call | solution.py:633
  330.6 90.8 %shard_map.87 = (bf16[8,2560]{1,0:T(8,128)(2,1)}, bf16[8,2560]{1,0:T(8,128)(2,1)}, bf16[3,8,896]{2,1,0:T(8,128)(2,1)}) custom-call(bf16[2048,896]{1,0:T(8,128)(2,1)} %get-tuple-element.56.refs_0_, bf16[2048,896]{1,0:T(8,128)(2,1)} %get-tuple-element.49.refs_6_.refs_1_, bf16[2048,2560]{1,0:T(8,128)(2,1)} %get-tuple-element.57.refs_2_, ...), custom_call_target="tpu_custom_call" | custom-call | tf_op jit(solution)/shard_map/pallas_call | solution.py:633
  421.4 0.8 slice_bitcast_fusion.5
  422.1 0.8 slice_bitcast_fusion.3
  422.9 0.8 slice_bitcast_fusion.4
  423.7 0.7 copy.21
  424.4 0.8 slice_bitcast_fusion.2
  425.2 0.7 copy.22
  425.9 0.8 slice_bitcast_fusion.1
  426.7 0.8 slice_bitcast_fusion
  427.5 0.7 copy.23
  428.2 4.2 copy.37
  (6 shorter events, 0.1 us)
